TPU v7x, 512 devices: a whole 4x4x16 slice. The times are simulated.
512 devices in a mesh: orb: 64 (over z, y), fft: 8 (over x, core).
Axes of the slice: x: 4, y: 4, z: 16, core: 2. Of those that a mesh axis runs over, the one named last changes fastest.
Arguments:
- orbitals: bfloat16 [512, 256, 256], P('orb', 'fft'), may hold values from -6 to 6
- kernel: float32 [256, 256], P('fft'), may hold values from 0.02 to 2
- partner_owner: int32 [512, 2, 1], P('orb'), may hold values from 0 to 63; in each aligned block of 16 rows (0 to 15, 16 to 31, ..., all dimensions but the last counted through in order) at most 2 rows name the same one
- partner_local: int32 [512, 2], P('orb'), may hold values from 0 to 7
Outputs:
- exchange_term: float32 [512, 256, 256], P('orb', 'fft')
Inputs may be any that keep to these rules, and one draw needn't show every extreme that they name: `partner_owner`: among the 16 partners named on one index of orb, no owner is named more than 2 times, a bound that some block reaches; every owner is named somewhere.
All inputs are finite; a program needn't handle non-finite values.
Results may differ from a plain program's by a relative error of at most 0.0004.
Values may be sent and summed in bfloat16 or wider, within the bound.
No kernel may reach another device: no remote copies, remote signals or barrier semaphores. Data moves between devices by JAX's collectives and lax.ppermute only.
A program may use at most 64 MiB of HBM per device.

v0:
```python
import math

import jax
import jax.numpy as jnp
from jax import lax
from jax.sharding import PartitionSpec as P


def sent_to_all(x, axis):
    count = lax.axis_size(axis)
    return lax.all_to_all(jnp.broadcast_to(x[None], (count, *x.shape)), axis, 0, 0, tiled=True)


def in_order(tiles, dim):
    tiles = jnp.moveaxis(tiles, 0, dim)
    shape = tiles.shape
    return tiles.reshape(*shape[:dim], shape[dim] * shape[dim + 1], *shape[dim + 2 :])


def gathered_copies(x, axis, dim):
    tiles = sent_to_all(x, axis)
    return in_order(tiles, dim)


def tables(length):
    series = jnp.arange(length, dtype=jnp.int32)
    phase = series[:, None] * series[None, :] % length
    angle = phase.astype(jnp.float32) * (2.0 * math.pi / length)
    return (jnp.cos(angle), jnp.sin(angle))


def product(form, left, right):
    return jnp.einsum(form, left, right, precision=lax.Precision.HIGHEST)


def group_potential(density, kernel):
    grouped = lax.all_to_all(density, "fft", split_axis=0, concat_axis=1, tiled=True)
    whole = gathered_copies(kernel, "fft", 0)
    full_x = grouped.shape[1]
    width_y = grouped.shape[2]
    cos_y, sin_y = tables(width_y)
    cos_x, sin_x = tables(full_x)
    real_y = product("txy,yk->txk", grouped, cos_y)
    imag_y = -product("txy,yk->txk", grouped, sin_y)
    f_real = product("txk,xq->tqk", real_y, cos_x) + product("txk,xq->tqk", imag_y, sin_x)
    f_imag = product("txk,xq->tqk", imag_y, cos_x) - product("txk,xq->tqk", real_y, sin_x)
    weight = whole.T
    g_real = weight[None] * f_real
    g_imag = weight[None] * f_imag
    h_real = product("tqk,qx->txk", g_real, cos_x) - product("tqk,qx->txk", g_imag, sin_x)
    h_imag = product("tqk,qx->txk", g_real, sin_x) + product("tqk,qx->txk", g_imag, cos_x)
    spread = product("txk,ky->txy", h_real, cos_y) - product("txk,ky->txy", h_imag, sin_y)
    spread = spread / (full_x * width_y)
    return lax.all_to_all(spread, "fft", split_axis=1, concat_axis=0, tiled=True)


def on_device(orbitals, kernel, partner_owner, partner_local):
    peer_count = lax.axis_size("orb")
    orb_dev, rows_x, width_y = orbitals.shape
    task_count = partner_local.shape[0]
    wanted_count = 2 * task_count
    capacity = max(2, (4 * task_count + peer_count - 1) // peer_count)
    owner_ids = partner_owner.reshape(wanted_count)
    local_ids = partner_local.reshape(wanted_count)
    peer_ids = jnp.arange(peer_count, dtype=jnp.int32)
    owner_hot = (owner_ids[:, None] == peer_ids[None, :]).astype(jnp.int32)
    earlier = jnp.cumsum(owner_hot, axis=0) - owner_hot
    position = jnp.sum(earlier * owner_hot, axis=1)
    target = owner_ids * capacity + position
    slot_ids = jnp.arange(peer_count * capacity, dtype=jnp.int32)
    placed = target[:, None] == slot_ids[None, :]
    wanted = jnp.max(jnp.where(placed, local_ids[:, None], -1), axis=0).reshape(
        peer_count, capacity
    )
    asked = lax.all_to_all(wanted, "orb", split_axis=0, concat_axis=0, tiled=True)
    flat_asked = asked.reshape(peer_count * capacity)
    present = flat_asked >= 0
    picked = jnp.take(orbitals, jnp.clip(flat_asked, 0, orb_dev - 1), axis=0)
    served = jnp.where(present[:, None, None], picked, jnp.zeros_like(picked))
    served = served.reshape(peer_count, capacity, rows_x, width_y)
    arrived = lax.all_to_all(served, "orb", split_axis=0, concat_axis=0, tiled=True)
    arrived = arrived.reshape(peer_count * capacity, rows_x, width_y)
    chosen = (
        jnp.take(arrived, target, axis=0)
        .reshape(task_count, 2, rows_x, width_y)
        .astype(jnp.float32)
    )
    left_orbital = chosen[:, 0]
    right_orbital = chosen[:, 1]
    density = left_orbital * right_orbital
    potential = group_potential(density, kernel)
    contrib = jnp.stack([potential * right_orbital, potential * left_orbital], axis=1)
    contrib = contrib.reshape(wanted_count, rows_x, width_y)
    outgoing = (
        jnp.zeros((peer_count * capacity, rows_x, width_y), jnp.float32).at[target].set(contrib)
    )
    outgoing = outgoing.reshape(peer_count, capacity, rows_x, width_y)
    incoming = lax.all_to_all(outgoing, "orb", split_axis=0, concat_axis=0, tiled=True)
    incoming = incoming.reshape(peer_count * capacity, rows_x * width_y)
    select = (flat_asked[None, :] == jnp.arange(orb_dev, dtype=jnp.int32)[:, None]).astype(
        jnp.float32
    )
    total = jnp.dot(select, incoming, precision=lax.Precision.HIGHEST)
    return (-total).reshape(orb_dev, rows_x, width_y)


def solution(mesh):
    in_specs = (P("orb", "fft", None), P("fft", None), P("orb", None, None), P("orb", None))
    out_specs = P("orb", "fft", None)
    return jax.shard_map(
        on_device, mesh=mesh, in_specs=in_specs, out_specs=out_specs, check_vma=False
    )
```

profile of v0, /device:TPU:8, one launch (start us, length us, event | category | flops | bytes accessed | tf_op | source)
XLA Modules:
  0.0 404.2 jit_solution(12548411028635859213)
XLA Ops:
  0.0 0.8 copy.55
  0.9 0.8 copy.54
  1.8 0.2 select_reduce_fusion.1
  2.0 0.1 select_reduce_fusion
  2.1 0.1 all_to_all.31
  2.3 32.3 %all_to_all.45 = s32[64,1,2]{2,1,0:T(1,128)S(1)} all-to-all(s32[64,1,2]{2,1,0:T(1,128)S(1)} %bitcast.64), channel_id=1, replica_groups=mesh['orb'=64,'fft'=8] {'orb'}, dimensions={0} | all-to-all | bytes 1024 | tf_op jit(solution)/shard_map/all_to_all | solution.py:75
  34.7 0.1 copy.62
  34.8 0.1 copy.64
  34.9 0.1 copy.65
  35.0 0.1 min.18
  35.2 0.7 gather_fusion
  35.9 1.6 select_select_fusion
  37.5 5.5 %all-to-all-start.2 = ((bf16[64,2,32,256]{3,2,1,0:T(8,128)(2,1)}), bf16[64,2,32,256]{3,2,1,0:T(8,128)(2,1)S(1)}, u32[]{:S(2)}, u32[]{:S(2)}) async-start(bf16[64,2,32,256]{3,2,1,0:T(8,128)(2,1)} %select_select_fusion), calls=%async_computation.2 | async-start | bytes 4194304 | tf_op jit(solution)/shard_map/all_to_all | solution.py:81
  43.4 0.1 copy.60
  43.5 98.6 %all-to-all-done.2 = bf16[64,2,32,256]{3,2,1,0:T(8,128)(2,1)S(1)} async-done(((bf16[64,2,32,256]{3,2,1,0:T(8,128)(2,1)}), bf16[64,2,32,256]{3,2,1,0:T(8,128)(2,1)S(1)}, u32[]{:S(2)}, u32[]{:S(2)}) %all-to-all-start.2) | async-done | bytes 2097184 | tf_op jit(solution)/shard_map/all_to_all | solution.py:81
  142.1 0.7 broadcast_in_dim.70
  142.8 4.3 %all-to-all-start.1 = ((f32[8,32,256]{2,1,0:T(8,128)}), f32[8,32,256]{2,1,0:T(8,128)S(1)}, u32[]{:S(2)}, u32[]{:S(2)}) async-start(f32[8,32,256]{2,1,0:T(8,128)} %broadcast_in_dim.70), calls=%async_computation.1 | async-start | bytes 524288 | tf_op jit(solution)/shard_map/all_to_all | solution.py:11
  147.1 0.6 gather_fusion.1
  147.7 0.1 select_convert_fusion
  147.8 0.7 multiply_bitcast_fusion
  148.6 6.1 %all-to-all-done.1 = f32[8,32,256]{2,1,0:T(8,128)S(1)} async-done(((f32[8,32,256]{2,1,0:T(8,128)}), f32[8,32,256]{2,1,0:T(8,128)S(1)}, u32[]{:S(2)}, u32[]{:S(2)}) %all-to-all-start.1) | async-done | bytes 262176 | tf_op jit(solution)/shard_map/all_to_all | solution.py:11
  154.6 3.6 all-to-all-start.3
  158.2 0.1 copy.58
  158.4 7.1 %all-to-all-done.3 = f32[8,32,256]{2,1,0:T(8,128)S(1)} async-done(((f32[8,32,256]{2,1,0:T(8,128)}), f32[8,32,256]{2,1,0:T(8,128)S(1)}, u32[]{:S(2)}, u32[]{:S(2)}) %all-to-all-start.3) | async-done | bytes 262176 | tf_op jit(solution)/shard_map/all_to_all | solution.py:37
  165.5 1.4 convolution_negate_fusion.1
  166.9 1.3 fusion.21
  168.2 1.8 fusion.19
  170.0 1.8 fusion.15
  171.8 1.8 fusion.3
  173.5 1.8 fusion.24
  175.3 1.8 fusion.17
  177.1 1.8 fusion.2
  178.9 1.8 convolution_subtract_fusion.1
  180.6 2.0 convolution_add_fusion
  182.6 1.3 fusion.13
  184.0 1.4 fusion.1
  185.4 0.3 copy.66
  185.6 9.9 %all_to_all.46 = f32[1,256,256]{2,0,1:T(1,128)S(1)} all-to-all(f32[1,256,256]{2,0,1:T(1,128)S(1)} %copy.66), channel_id=1, replica_groups=mesh['orb'=64,'fft'=8] {'fft'}, dimensions={1} | all-to-all | bytes 524288 | tf_op jit(solution)/shard_map/all_to_all | solution.py:54
  195.7 2.5 broadcast_in_dim.69
  198.2 2.6 scatter_fusion
  200.7 6.1 %all-to-all-start.5 = ((f32[64,2,32,256]{3,2,1,0:T(8,128)}), f32[64,2,32,256]{3,2,1,0:T(8,128)}, u32[]{:S(2)}, u32[]{:S(2)}) async-start(f32[64,2,32,256]{3,2,1,0:T(8,128)} %bitcast.53), calls=%async_computation.5 | async-start | bytes 8388608 | tf_op jit(solution)/shard_map/all_to_all | solution.py:98
  206.9 0.5 broadcast.212
  207.4 0.7 reduce.3
  208.1 0.1 eq.50
  208.3 188.2 %all-to-all-done.5 = f32[64,2,32,256]{3,2,1,0:T(8,128)} async-done(((f32[64,2,32,256]{3,2,1,0:T(8,128)}), f32[64,2,32,256]{3,2,1,0:T(8,128)}, u32[]{:S(2)}, u32[]{:S(2)}) %all-to-all-start.5) | async-done | bytes 4194336 | tf_op jit(solution)/shard_map/all_to_all | solution.py:98
  396.5 5.5 %copy.69 = f32[16,8,32,256]{3,1,2,0:T(8,128)S(1)} copy(f32[16,8,32,256]{3,2,1,0:T(8,128)} %bitcast.23) | data formatting | bytes 8388608
  402.0 1.5 convolution_negate_fusion
  403.4 0.8 copy.67
  (28 shorter events, 0.9 us)
Async XLA Ops:
  0.0 35.2 %copy-start = (bf16[8,32,256]{2,1,0:T(8,128)(2,1)S(1)}, bf16[8,32,256]{2,1,0:T(8,128)(2,1)}, u32[]{:S(2)}) copy-start(bf16[8,32,256]{2,1,0:T(8,128)(2,1)} %param.4) | copy-start | bytes 393220
  37.5 5.6 %copy-start.2 = (s32[8,2,1]{0,2,1:T(1,128)S(1)}, s32[8,2,1]{0,2,1:T(1,128)}, u32[]{:S(2)}) copy-start(s32[8,2,1]{0,2,1:T(1,128)} %param.6) | copy-start | bytes 196
  37.5 104.6 %copy-start.1 = (f32[32,256]{1,0:T(8,128)S(1)}, f32[32,256]{1,0:T(8,128)}, u32[]{:S(2)}) copy-start(f32[32,256]{1,0:T(8,128)} %param.5) | copy-start | bytes 98308
  37.5 104.6 %all-to-all-start.2 = ((bf16[64,2,32,256]{3,2,1,0:T(8,128)(2,1)}), bf16[64,2,32,256]{3,2,1,0:T(8,128)(2,1)S(1)}, u32[]{:S(2)}, u32[]{:S(2)}) async-start(bf16[64,2,32,256]{3,2,1,0:T(8,128)(2,1)} %select_select_fusion), calls=%async_computation.2 | async-start | bytes 4194304 | tf_op jit(solution)/shard_map/all_to_all | solution.py:81
  142.8 11.8 %all-to-all-start.1 = ((f32[8,32,256]{2,1,0:T(8,128)}), f32[8,32,256]{2,1,0:T(8,128)S(1)}, u32[]{:S(2)}, u32[]{:S(2)}) async-start(f32[8,32,256]{2,1,0:T(8,128)} %broadcast_in_dim.70), calls=%async_computation.1 | async-start | bytes 524288 | tf_op jit(solution)/shard_map/all_to_all | solution.py:11
  154.6 10.9 %all-to-all-start.3 = ((f32[8,32,256]{2,1,0:T(8,128)}), f32[8,32,256]{2,1,0:T(8,128)S(1)}, u32[]{:S(2)}, u32[]{:S(2)}) async-start(f32[8,32,256]{2,1,0:T(8,128)} %multiply_bitcast_fusion), calls=%async_computation.3 | async-start | bytes 524288 | tf_op jit(solution)/shard_map/all_to_all | solution.py:37
  200.7 195.7 %all-to-all-start.5 = ((f32[64,2,32,256]{3,2,1,0:T(8,128)}), f32[64,2,32,256]{3,2,1,0:T(8,128)}, u32[]{:S(2)}, u32[]{:S(2)}) async-start(f32[64,2,32,256]{3,2,1,0:T(8,128)} %bitcast.53), calls=%async_computation.5 | async-start | bytes 8388608 | tf_op jit(solution)/shard_map/all_to_all | solution.py:98
where the time goes:
time: 405 us; the launch traced here: 404 us
  waiting for transfers between devices  300 us (74%)
  blocking collectives  42.3 us (10%)
  matrix products  21.3 us (5%)
  starting transfers between devices  19.6 us (5%)
  local copies, waits for them, and re-layouts  17.2 us (4%)
    all_to_all x1, waiting for transfers between devices, on_device(): lax.all_to_all(outgoing, 'orb', split_axis=0, concat_axis=0, tiled=True)  188 us
    all_to_all x1, waiting for transfers between devices, on_device(): lax.all_to_all(served, 'orb', split_axis=0, concat_axis=0, tiled=True)  98.6 us
    all_to_all x1, blocking collectives, on_device(): lax.all_to_all(wanted, 'orb', split_axis=0, concat_axis=0, tiled=True)  32.3 us
    dot_general x12, matrix products, product(): return jnp.einsum(form, left, right, precision=lax.Precision.HIGHEST)  19.8 us
    all_to_all x1, blocking collectives, group_potential(): lax.all_to_all(spread, 'fft', split_axis=1, concat_axis=0, tiled=True)  9.91 us
  transfers between devices with their start and end apart: 4, of which 4 were waited for; matrix products, arithmetic and copies ran while one was open for 1% of the time, Pallas kernels for 0%

commit v1 on v0

v1 whole, which is shorter than its diff:
```python
import math

import jax
import jax.numpy as jnp
import numpy as np
from jax import lax
from jax.experimental import pallas as pl
from jax.experimental.pallas import tpu as pltpu
from jax.sharding import Mesh
from jax.sharding import PartitionSpec as P

Z, Y = 16, 4


def tables(length):
    series = np.arange(length, dtype=np.int64)
    angle = (series[:, None] * series[None, :] % length) * (2.0 * math.pi / length)
    return np.cos(angle).astype(np.float32), np.sin(angle).astype(np.float32)


def halves(a):
    high = a.astype(jnp.bfloat16)
    low = (a - high.astype(jnp.float32)).astype(jnp.bfloat16)
    return high, low


def mul(a, b):
    return jnp.dot(a, b, preferred_element_type=jnp.float32)


def mul3(a, b):
    return mul(a[0], b[0]) + (mul(a[0], b[1]) + mul(a[1], b[0]))


def transform_kernel(grid_ref, weight_ref, cs_high, cs_low, out_ref):
    n = grid_ref.shape[0]
    row = (cs_high[:, :], cs_low[:, :])
    cos = (cs_high[:, :n], cs_low[:, :n])
    sin = (cs_high[:, n:], cs_low[:, n:])
    weight = weight_ref[...].T * (1.0 / (n * n))
    u = halves(mul3(halves(grid_ref[...]), row))
    p = mul3(cos, u)
    q = mul3(sin, u)
    h_real = halves((p[:, :n] - q[:, n:]) * weight)
    h_imag = halves((p[:, n:] + q[:, :n]) * weight)
    g_real = halves(mul3(cos, h_real) + mul3(sin, h_imag))
    g_imag = halves(mul3(sin, h_real) - mul3(cos, h_imag))
    out_ref[...] = mul3(g_real, cos) - mul3(g_imag, sin)


def potential_of(grid, weight):
    n = grid.shape[0]
    both = np.concatenate(tables(n), axis=1)
    high = both.astype(jnp.bfloat16)
    low = (both - high.astype(np.float32)).astype(jnp.bfloat16)
    return pl.pallas_call(
        transform_kernel,
        out_shape=jax.ShapeDtypeStruct((n, n), jnp.float32),
        name="potential",
    )(grid, weight, jnp.asarray(high), jnp.asarray(low))


def swap(x, axis):
    return lax.all_to_all(x, axis, split_axis=0, concat_axis=0, tiled=True)


def on_device(orbitals, kernel, partner_owner, partner_local):
    orb_dev, rows_x, width_y = orbitals.shape
    tasks = partner_local.shape[0]
    fft = lax.axis_size("fft")
    own_y = lax.axis_index("y")
    rows = rows_x // Z
    points = rows * width_y
    lines = orb_dev * points // 128
    named = jnp.concatenate([partner_owner.reshape(-1), partner_local.reshape(-1)])
    named = jnp.pad(named.astype(jnp.bfloat16)[None], ((0, 7), (0, 128 - 4 * tasks)))
    cut = orbitals.reshape(orb_dev, Z, rows, width_y // 128, 128)
    cut = cut.transpose(1, 0, 2, 3, 4).reshape(Z, lines, 128)
    cut = jnp.concatenate([cut, jnp.broadcast_to(named[None], (Z, 8, 128))], axis=1)
    column = swap(cut, "z")
    every = swap(jnp.broadcast_to(column[None], (Y, *column.shape)), "y")
    table = every[:, :, :lines].reshape(Y * Z * orb_dev, points)
    names = column[:, lines, : 4 * tasks].astype(jnp.int32)
    owner = names[:, : 2 * tasks].reshape(Z * tasks, 2)
    local = names[:, 2 * tasks :].reshape(Z * tasks, 2)
    place = (owner % Y) * (Z * orb_dev) + (owner // Y) * orb_dev + local
    place = place.T.reshape(2 * Z * tasks)
    total = Y * Z * orb_dev
    pick = (place[:, None] == jnp.arange(total, dtype=jnp.int32)[None]).astype(jnp.bfloat16)
    chosen = jnp.dot(pick, table, preferred_element_type=jnp.float32)
    left, right = chosen[: Z * tasks], chosen[Z * tasks :]
    density = (left * right).reshape(Z, tasks, points)
    slab = swap(density, "z")
    slab = slab.reshape(Z, tasks, rows, width_y).transpose(1, 0, 2, 3)
    slab = slab.reshape(fft, rows_x, width_y)
    slab = jnp.concatenate([slab, jnp.broadcast_to(kernel[None], (fft, *kernel.shape))], axis=1)
    full = swap(slab, "fft")
    grid = full[:, :rows_x].reshape(fft * rows_x, width_y)
    weight = full[:, rows_x:].reshape(fft * kernel.shape[0], kernel.shape[1])
    spread = potential_of(grid, weight).reshape(fft, rows_x, width_y)
    back = swap(spread, "fft")
    back = back.reshape(tasks, Z, rows, width_y).transpose(1, 0, 2, 3).reshape(Z, tasks, points)
    potential = swap(back, "z").reshape(Z * tasks, points)
    contrib = jnp.concatenate([potential * right, potential * left], axis=0)
    place_hot = (jnp.arange(total, dtype=jnp.int32)[:, None] == place[None]).astype(jnp.float32)
    summed = -jnp.dot(place_hot, contrib, precision=lax.Precision.HIGHEST)
    summed = swap(summed.reshape(Y, Z * orb_dev, points), "y").sum(0)
    home = swap(summed.reshape(Z, orb_dev, points), "z")
    home = home.reshape(Z, orb_dev, rows, width_y).transpose(1, 0, 2, 3)
    return home.reshape(orb_dev, rows_x, width_y)


def solution(mesh):
    devices = mesh.devices.reshape(Z, Y, mesh.devices.shape[1])
    fine = Mesh(devices, ("z", "y", "fft"))
    orb = ("z", "y")
    in_specs = (P(orb, "fft", None), P("fft", None), P(orb, None, None), P(orb, None))
    out_specs = P(orb, "fft", None)
    return jax.shard_map(
        on_device, mesh=fine, in_specs=in_specs, out_specs=out_specs, check_vma=False
    )
```

time: 405 us -> 169 us (0.42)
  the two profiles are of different devices: /device:TPU:8 before, /device:TPU:32 now
where the time goes in v1:
time: 169 us; the launch traced here: 168 us
  blocking collectives  144 us (85%)
  waiting for transfers between devices  8.64 us (5%)
  local copies, waits for them, and re-layouts  5.77 us (3%)
  starting transfers between devices  4.46 us (3%)
  Pallas kernels  3.64 us (2%)
    all_to_all x7, blocking collectives, swap(): return lax.all_to_all(x, axis, split_axis=0, concat_axis=0, tiled=True)  144 us
    all_to_all x1, waiting for transfers between devices, swap(): return lax.all_to_all(x, axis, split_axis=0, concat_axis=0, tiled=True)  8.64 us
    all_to_all x1, starting transfers between devices, swap(): return lax.all_to_all(x, axis, split_axis=0, concat_axis=0, tiled=True)  4.46 us
    pallas_call x1, Pallas kernels, potential_of(): pl.pallas_call(transform_kernel, out_shape=jax.ShapeDtypeStruct((n, n), j...  3.64 us
  transfers between devices with their start and end apart: 1, of which 1 were waited for; matrix products, arithmetic and copies ran while one was open for 0% of the time, Pallas kernels for 0%

profile of v1, /device:TPU:32, one launch (start us, length us, event | category | flops | bytes accessed | tf_op | source)
XLA Modules:
  0.0 168.3 jit_solution(135272196105392504)
XLA Ops:
  0.0 0.0 copy-start.1
  0.0 0.7 convert.10
  0.7 0.0 copy-done.1
  0.7 0.1 copy.27
  0.8 0.1 concatenate.24
  0.9 0.1 copy.28
  1.0 0.1 concatenate.25
  1.1 0.9 reshape.96
  2.1 0.1 fusion.20
  2.2 30.1 %all_to_all.40 = bf16[16,40,128]{2,1,0:T(8,128)(2,1)S(1)} all-to-all(bf16[16,40,128]{2,1,0:T(8,128)(2,1)S(1)} %copy.29), channel_id=1, replica_groups=mesh['z'=16,'y'=4,'fft'=8] {'z'}, dimensions={0} | all-to-all | bytes 327680 | tf_op jit(solution)/shard_map/all_to_all | solution.py:64
  32.3 0.9 broadcast_in_dim.7
  33.3 4.5 %all-to-all-start.1 = ((bf16[4,16,40,128]{3,2,1,0:T(8,128)(2,1)}), bf16[4,16,40,128]{3,2,1,0:T(8,128)(2,1)S(1)}, u32[]{:S(2)}, u32[]{:S(2)}) async-start(bf16[4,16,40,128]{3,2,1,0:T(8,128)(2,1)} %broadcast_in_dim.7), calls=%async_computation.1 | async-start | bytes 1310720 | tf_op jit(solution)/shard_map/all_to_all | solution.py:64
  37.7 0.1 fusion.23
  37.8 0.1 reshape.98
  37.9 0.1 reshape.99
  38.0 0.1 fusion.9
  38.1 0.1 copy.30
  38.1 8.6 %all-to-all-done.1 = bf16[4,16,40,128]{3,2,1,0:T(8,128)(2,1)S(1)} async-done(((bf16[4,16,40,128]{3,2,1,0:T(8,128)(2,1)}), bf16[4,16,40,128]{3,2,1,0:T(8,128)(2,1)S(1)}, u32[]{:S(2)}, u32[]{:S(2)}) %all-to-all-start.1) | async-done | bytes 655392 | tf_op jit(solution)/shard_map/all_to_all | solution.py:64
  46.8 0.3 reshape.100
  47.1 0.3 fusion.3
  47.5 24.1 %all_to_all.41 = f32[16,8,512]{2,1,0:T(8,128)S(1)} all-to-all(f32[16,8,512]{2,1,0:T(8,128)S(1)} %multiply_bitcast_fusion), channel_id=1, replica_groups=mesh['z'=16,'y'=4,'fft'=8] {'z'}, dimensions={0} | all-to-all | bytes 524288 | tf_op jit(solution)/shard_map/all_to_all | solution.py:64
  71.6 0.1 copy.36
  71.8 0.0 copy-start
  71.8 0.2 reshape.103
  72.0 0.6 copy-done
  72.6 14.5 %all_to_all.42 = f32[8,64,256]{2,1,0:T(8,128)S(1)} all-to-all(f32[8,64,256]{2,1,0:T(8,128)S(1)} %pad_maximum_fusion), channel_id=1, replica_groups=mesh['z'=16,'y'=4,'fft'=8] {'fft'}, dimensions={0} | all-to-all | bytes 1048576 | tf_op jit(solution)/shard_map/all_to_all | solution.py:64
  87.1 0.8 fusion.22
  87.9 3.6 %potential.1 = f32[256,256]{1,0:T(8,128)} custom-call(f32[256,256]{1,0:T(8,128)} %bitcast.36, f32[256,256]{1,0:T(8,128)} %bitcast.35, bf16[256,512]{1,0:T(8,128)(2,1)} %constant.41.clone.cs_high, bf16[256,512]{1,0:T(8,128)(2,1)} %constant.42.clone.cs_low), custom_call_target="tpu_custom_call" | custom-call | tf_op jit(solution)/shard_map/potential/pallas_call | solution.py:56
  91.5 10.8 %all_to_all.43 = f32[8,32,256]{2,1,0:T(8,128)S(1)} all-to-all(f32[8,32,256]{2,1,0:T(8,128)} %bitcast.33), channel_id=1, replica_groups=mesh['z'=16,'y'=4,'fft'=8] {'fft'}, dimensions={0} | all-to-all | bytes 524288 | tf_op jit(solution)/shard_map/all_to_all | solution.py:64
  102.4 0.1 reshape.107
  102.5 0.2 copy.32
  102.7 22.8 %all_to_all.44 = f32[16,8,512]{2,1,0:T(8,128)S(1)} all-to-all(f32[16,8,512]{2,1,0:T(8,128)S(1)} %bitcast.40), channel_id=1, replica_groups=mesh['z'=16,'y'=4,'fft'=8] {'z'}, dimensions={0} | all-to-all | bytes 524288 | tf_op jit(solution)/shard_map/all_to_all | solution.py:64
  125.5 0.1 bitcast_multiply_fusion.1
  125.6 0.6 convolution_negate_fusion
  126.2 17.0 %all_to_all.45 = f32[4,128,512]{2,1,0:T(8,128)S(1)} all-to-all(f32[4,128,512]{2,1,0:T(8,128)S(1)} %bitcast.32), channel_id=1, replica_groups=mesh['z'=16,'y'=4,'fft'=8] {'y'}, dimensions={0} | all-to-all | bytes 2097152 | tf_op jit(solution)/shard_map/all_to_all | solution.py:64
  143.2 0.1 reduce_sum.9
  143.3 24.3 %all_to_all.46 = f32[16,8,512]{2,1,0:T(8,128)S(1)} all-to-all(f32[16,8,512]{2,1,0:T(8,128)S(1)} %bitcast.34), channel_id=1, replica_groups=mesh['z'=16,'y'=4,'fft'=8] {'z'}, dimensions={0} | all-to-all | bytes 524288 | tf_op jit(solution)/shard_map/all_to_all | solution.py:64
  167.6 0.8 copy.34
  (10 shorter events, 0.2 us)
Async XLA Ops:
  0.0 0.7 copy-start.1
  33.3 13.5 %all-to-all-start.1 = ((bf16[4,16,40,128]{3,2,1,0:T(8,128)(2,1)}), bf16[4,16,40,128]{3,2,1,0:T(8,128)(2,1)S(1)}, u32[]{:S(2)}, u32[]{:S(2)}) async-start(bf16[4,16,40,128]{3,2,1,0:T(8,128)(2,1)} %broadcast_in_dim.7), calls=%async_computation.1 | async-start | bytes 1310720 | tf_op jit(solution)/shard_map/all_to_all | solution.py:64
  71.8 0.8 copy-start

commit v2 on v1

v2 whole, which is shorter than its diff:
```python
import math

import jax
import jax.numpy as jnp
import numpy as np
from jax import lax
from jax.experimental import pallas as pl
from jax.experimental.pallas import tpu as pltpu
from jax.sharding import Mesh
from jax.sharding import PartitionSpec as P

Z, Y = 16, 4
LANES = 128
TOP = 32767.0
STEPS = 128.0
FLOOR = 1e-37
KERNEL_LOW, KERNEL_HIGH = 0.02, 2.0
KERNEL_MID = 0.5 * (math.log(KERNEL_HIGH) + math.log(KERNEL_LOW))
KERNEL_STEP = 0.5 * (math.log(KERNEL_HIGH) - math.log(KERNEL_LOW)) / TOP


def tables(length):
    series = np.arange(length, dtype=np.int64)
    angle = (series[:, None] * series[None, :] % length) * (2.0 * math.pi / length)
    return np.cos(angle).astype(np.float32), np.sin(angle).astype(np.float32)


def level_of(largest):
    return jnp.ceil(jnp.log(jnp.maximum(largest, FLOOR)) * (STEPS / math.log(2.0))) + 1.0


def coded(values, level):
    share = jnp.sqrt(jnp.abs(values) * jnp.exp(level * (-math.log(2.0) / STEPS)))
    share = jnp.round(jnp.minimum(share, 1.0) * TOP)
    return jnp.where(values < 0, -share, share)


def decoded(codes, level):
    share = codes * (1.0 / TOP)
    return share * jnp.abs(share) * jnp.exp(level * (math.log(2.0) / STEPS))


def to_16(codes):
    return codes.astype(jnp.int32).astype(jnp.int16)


def from_16(codes):
    return codes.astype(jnp.int32).astype(jnp.float32)


def coded_rows(values):
    level = level_of(jnp.max(jnp.abs(values), axis=1, keepdims=True))
    behind = jnp.broadcast_to(level, (values.shape[0], LANES))
    return to_16(jnp.concatenate([coded(values, level), behind], axis=1))


def decoded_rows(codes, points):
    wide = from_16(codes)
    return decoded(wide[..., :points], wide[..., points : points + 1])


def halves(a):
    high = a.astype(jnp.bfloat16)
    low = (a - high.astype(jnp.float32)).astype(jnp.bfloat16)
    return high, low


def mul(a, b):
    return jnp.dot(a, b, preferred_element_type=jnp.float32)


def mul3(a, b):
    return mul(a[0], b[0]) + (mul(a[0], b[1]) + mul(a[1], b[0]))


def transform_kernel(data_ref, cs_high, cs_low, out_ref):
    n = data_ref.shape[2]
    slabs = data_ref.shape[0]
    rows = n // slabs
    data = from_16(data_ref[...])
    level = data[:, rows : rows + 8][:, None]
    grid = decoded(data[:, :rows].reshape(slabs, rows // 8, 8, n), level).reshape(n, n)
    weight = jnp.exp(data[:, rows + 8 :].reshape(n, n) * KERNEL_STEP + KERNEL_MID)
    weight = weight.T * (1.0 / (n * n))
    row = (cs_high[:, :], cs_low[:, :])
    cos = (cs_high[:, :n], cs_low[:, :n])
    sin = (cs_high[:, n:], cs_low[:, n:])
    u = halves(mul3(halves(grid), row))
    p = mul3(cos, u)
    q = mul3(sin, u)
    h_real = halves((p[:, :n] - q[:, n:]) * weight)
    h_imag = halves((p[:, n:] + q[:, :n]) * weight)
    g_real = halves(mul3(cos, h_real) + mul3(sin, h_imag))
    g_imag = halves(mul3(sin, h_real) - mul3(cos, h_imag))
    spread = mul3(g_real, cos) - mul3(g_imag, sin)
    level = level_of(jnp.max(jnp.abs(spread), axis=(0, 1), keepdims=True))
    codes = coded(spread, level).reshape(slabs, rows, n)
    behind = jnp.broadcast_to(level[None], (slabs, 8, n))
    out_ref[...] = to_16(jnp.concatenate([codes, behind], axis=1))


def potential_of(data):
    slabs, height, n = data.shape
    both = np.concatenate(tables(n), axis=1)
    high = both.astype(jnp.bfloat16)
    low = (both - high.astype(np.float32)).astype(jnp.bfloat16)
    return pl.pallas_call(
        transform_kernel,
        out_shape=jax.ShapeDtypeStruct((slabs, n // slabs + 8, n), jnp.int16),
        name="potential",
    )(data, jnp.asarray(high), jnp.asarray(low))


def swap(x, axis):
    return lax.all_to_all(x, axis, split_axis=0, concat_axis=0, tiled=True)


def to_all(x, axis):
    return swap(jnp.broadcast_to(x[None], (lax.axis_size(axis), *x.shape)), axis)


def pieces(slab):
    count, rows, width = slab.shape
    cut = slab.reshape(count, rows // 8, 8, width // LANES, LANES).transpose(2, 3, 0, 1, 4)
    return cut.reshape(Z, count, rows // 8 * LANES)


def whole(cut, width):
    count = cut.shape[1]
    slab = cut.reshape(8, width // LANES, count, -1, LANES).transpose(2, 3, 0, 1, 4)
    return slab.reshape(count, -1, width)


def on_device(orbitals, kernel, partner_owner, partner_local):
    orb_dev, rows_x, width_y = orbitals.shape
    tasks = partner_local.shape[0]
    points = rows_x * width_y // Z
    total = Y * Z * orb_dev
    own_y = lax.axis_index("y")
    named = jnp.concatenate([partner_owner[:, :, 0], partner_local], axis=1)
    named = jnp.pad(named.astype(jnp.bfloat16), ((0, 0), (0, LANES - 4)))
    behind = jnp.broadcast_to(named[None], (Z, tasks, LANES))
    column = swap(jnp.concatenate([pieces(orbitals), behind], axis=2), "z")
    every = to_all(column, "y").reshape(total, points + LANES)
    table = every[:, :points]

    def places(block):
        names = block[:, points : points + 4].astype(jnp.int32)
        owner = names[:, :2].T.reshape(-1)
        return (owner % Y * Z + owner // Y) * orb_dev + names[:, 2:].T.reshape(-1)

    def chosen(place):
        pick = place[:, None] == jnp.arange(total, dtype=jnp.int32)[None]
        return mul(pick.astype(jnp.bfloat16), table)

    own = chosen(places(column.reshape(Z * tasks, points + LANES)))
    density = coded_rows(own[: Z * tasks] * own[Z * tasks :])
    slab = whole(swap(density.reshape(Z, tasks, -1), "z"), width_y)
    weight = to_16(jnp.round((jnp.log(kernel) - KERNEL_MID) * (1.0 / KERNEL_STEP)))
    weight = jnp.broadcast_to(weight[None], (tasks, *weight.shape))
    full = swap(jnp.concatenate([slab, weight], axis=1), "fft")
    back = swap(potential_of(full), "fft")
    spread = to_all(swap(pieces(back), "z"), "y").reshape(total, -1)
    place = places(every)
    partner = chosen(jnp.concatenate([place[total:], place[:total]]))
    potential = decoded_rows(spread, points)
    contrib = (partner.reshape(2, total, points) * potential[None]).reshape(2 * total, points)
    mine = jnp.arange(Z * orb_dev, dtype=jnp.int32) + own_y * (Z * orb_dev)
    select = (mine[:, None] == place[None]).astype(jnp.bfloat16)
    high = lax.reduce_precision(contrib, 8, 7)
    low = (contrib - high).astype(jnp.bfloat16)
    summed = mul(select, high.astype(jnp.bfloat16)) + mul(select, low)
    home = swap(coded_rows(-summed).reshape(Z, orb_dev, -1), "z")
    return whole(decoded_rows(home, points), width_y)


def solution(mesh):
    devices = mesh.devices.reshape(Z, Y, mesh.devices.shape[1])
    fine = Mesh(devices, ("z", "y", "fft"))
    orb = ("z", "y")
    in_specs = (P(orb, "fft", None), P("fft", None), P(orb, None, None), P(orb, None))
    out_specs = P(orb, "fft", None)
    return jax.shard_map(
        on_device, mesh=fine, in_specs=in_specs, out_specs=out_specs, check_vma=False
    )
```

time: 169 us -> 154 us (0.911)
  blocking collectives: 144 us -> 72.6 us
  waiting for transfers between devices: 8.64 us -> 46.3 us
  starting transfers between devices: 4.46 us -> 19.3 us
  other arithmetic: 1.1 us -> 3.54 us
    all_to_all x7 -> x4, blocking collectives: 144 us -> 72.6 us  [swap(): return lax.all_to_all(x, axis, split_axis=0, concat_axis=0, tiled=True)]
    all_to_all x1 -> x4, waiting for transfers between devices: 8.64 us -> 46.3 us  [swap(): return lax.all_to_all(x, axis, split_axis=0, concat_axis=0, tiled=True)]
    all_to_all x1 -> x4, starting transfers between devices: 4.46 us -> 19.3 us  [swap(): return lax.all_to_all(x, axis, split_axis=0, concat_axis=0, tiled=True)]
    transpose x3 -> x6, local copies, waits for them, and re-layouts: 0.24 us -> 2.26 us  [the longest x1 0.99 us: pieces(): slab.reshape(count, rows // 8, 8, width // LANES, LANES)]
    reshape x8 -> x1, local copies, waits for them, and re-layouts: 2.67 us -> 0.71 us  [pieces(): slab.reshape(count, rows // 8, 8, width // LANES, LANES)]
  transfers between devices with their start and end apart: 1 -> 4, of which waited for: 1 -> 4; matrix products, arithmetic and copies ran while one was open for 0% -> 0% of each run, Pallas kernels for 0% -> 0%
where the time goes in v2:
time: 154 us; the launch traced here: 153 us
  blocking collectives  72.6 us (47%)
  waiting for transfers between devices  46.3 us (30%)
  starting transfers between devices  19.3 us (13%)
  local copies, waits for them, and re-layouts  5.45 us (4%)
  Pallas kernels  3.88 us (3%)
  other arithmetic  3.54 us (2%)
  matrix products  1.96 us (1%)
    all_to_all x4, blocking collectives, swap(): return lax.all_to_all(x, axis, split_axis=0, concat_axis=0, tiled=True)  72.6 us
    all_to_all x4, waiting for transfers between devices, swap(): return lax.all_to_all(x, axis, split_axis=0, concat_axis=0, tiled=True)  46.3 us
    all_to_all x4, starting transfers between devices, swap(): return lax.all_to_all(x, axis, split_axis=0, concat_axis=0, tiled=True)  19.3 us
    pallas_call x1, Pallas kernels, potential_of(): pl.pallas_call(transform_kernel, out_shape=jax.ShapeDtypeStruct((slabs, n...  3.88 us
  transfers between devices with their start and end apart: 4, of which 4 were waited for; matrix products, arithmetic and copies ran while one was open for 0% of the time, Pallas kernels for 0%

profile of v2, /device:TPU:32, one launch (start us, length us, event | category | flops | bytes accessed | tf_op | source)
XLA Modules:
  0.0 153.2 jit_solution(14722749856154688318)
XLA Ops:
  0.0 1.0 copy.42
  1.0 0.7 convert.7
  1.7 0.7 convert.8
  2.4 0.1 copy.55
  2.5 30.1 %all_to_all.40 = bf16[16,8,640]{2,1,0:T(8,128)(2,1)S(1)} all-to-all(bf16[16,8,640]{2,1,0:T(8,128)(2,1)S(1)} %pad_maximum_fusion), channel_id=1, replica_groups=mesh['z'=16,'y'=4,'fft'=8] {'z'}, dimensions={0} | all-to-all | bytes 327680 | tf_op jit(solution)/shard_map/all_to_all | solution.py:115
  32.6 0.9 broadcast_in_dim.13
  33.5 4.5 %all-to-all-start.1 = ((bf16[4,16,8,640]{3,2,1,0:T(8,128)(2,1)}), bf16[4,16,8,640]{3,2,1,0:T(8,128)(2,1)S(1)}, u32[]{:S(2)}, u32[]{:S(2)}) async-start(bf16[4,16,8,640]{3,2,1,0:T(8,128)(2,1)} %broadcast_in_dim.13), calls=%async_computation.1 | async-start | bytes 1310720 | tf_op jit(solution)/shard_map/all_to_all | solution.py:115
  38.0 0.1 copy.54
  38.1 8.9 %all-to-all-done.1 = bf16[4,16,8,640]{3,2,1,0:T(8,128)(2,1)S(1)} async-done(((bf16[4,16,8,640]{3,2,1,0:T(8,128)(2,1)}), bf16[4,16,8,640]{3,2,1,0:T(8,128)(2,1)S(1)}, u32[]{:S(2)}, u32[]{:S(2)}) %all-to-all-start.1) | async-done | bytes 655392 | tf_op jit(solution)/shard_map/all_to_all | solution.py:115
  47.0 0.3 fusion.8
  47.4 0.0 copy-start
  47.4 0.1 abs_reduce_fusion.1
  47.5 0.2 fusion.13
  47.7 0.1 reshape.251
  47.8 0.1 broadcast_in_dim.14
  47.9 0.7 fusion.11
  48.6 6.7 %all-to-all-start.2 = ((s16[16,8,640]{2,1,0:T(8,128)(2,1)}), s16[16,8,640]{2,1,0:T(8,128)(2,1)S(1)}, u32[]{:S(2)}, u32[]{:S(2)}) async-start(s16[16,8,640]{2,1,0:T(8,128)(2,1)} %fusion.11), calls=%async_computation.2 | async-start | bytes 327680 | tf_op jit(solution)/shard_map/all_to_all | solution.py:115
  55.3 0.0 copy-done
  55.3 14.1 %all-to-all-done.2 = s16[16,8,640]{2,1,0:T(8,128)(2,1)S(1)} async-done(((s16[16,8,640]{2,1,0:T(8,128)(2,1)}), s16[16,8,640]{2,1,0:T(8,128)(2,1)S(1)}, u32[]{:S(2)}, u32[]{:S(2)}) %all-to-all-start.2) | async-done | bytes 163872 | tf_op jit(solution)/shard_map/all_to_all | solution.py:115
  69.5 12.1 %all_to_all.41.data_ref = s16[8,72,256]{2,1,0:T(8,128)(2,1)} all-to-all(s16[8,72,256]{2,1,0:T(8,128)(2,1)S(1)} %pad_add_fusion), channel_id=1, replica_groups=mesh['z'=16,'y'=4,'fft'=8] {'fft'}, dimensions={0} | all-to-all | bytes 589824 | tf_op jit(solution)/shard_map/all_to_all | solution.py:115
  81.5 3.9 %potential.1 = s16[8,40,256]{2,1,0:T(8,128)(2,1)} custom-call(s16[8,72,256]{2,1,0:T(8,128)(2,1)} %all_to_all.41.data_ref, bf16[256,512]{1,0:T(8,128)(2,1)} %constant.93.clone.cs_high, bf16[256,512]{1,0:T(8,128)(2,1)} %constant.94.clone.cs_low), custom_call_target="tpu_custom_call" | custom-call | tf_op jit(solution)/shard_map/potential/pallas_call | solution.py:107
  85.4 9.7 %all_to_all.42 = s16[8,40,256]{2,1,0:T(8,128)(2,1)S(1)} all-to-all(s16[8,40,256]{2,1,0:T(8,128)(2,1)} %potential.1), channel_id=1, replica_groups=mesh['z'=16,'y'=4,'fft'=8] {'fft'}, dimensions={0} | all-to-all | bytes 327680 | tf_op jit(solution)/shard_map/all_to_all | solution.py:115
  95.2 0.7 copy.48
  95.9 4.7 %all-to-all-start.5 = ((s16[16,8,640]{2,1,0:T(8,128)(2,1)}), s16[16,8,640]{2,1,0:T(8,128)(2,1)S(1)}, u32[]{:S(2)}, u32[]{:S(2)}) async-start(s16[16,8,640]{2,1,0:T(8,128)(2,1)} %bitcast.18), calls=%async_computation.5 | async-start | bytes 327680 | tf_op jit(solution)/shard_map/all_to_all | solution.py:115
  100.6 0.1 slice_bitcast_fusion.1
  100.8 0.1 copy.44
  100.9 0.1 copy.45
  101.0 14.6 %all-to-all-done.5 = s16[16,8,640]{2,1,0:T(8,128)(2,1)S(1)} async-done(((s16[16,8,640]{2,1,0:T(8,128)(2,1)}), s16[16,8,640]{2,1,0:T(8,128)(2,1)S(1)}, u32[]{:S(2)}, u32[]{:S(2)}) %all-to-all-start.5) | async-done | bytes 163872 | tf_op jit(solution)/shard_map/all_to_all | solution.py:115
  115.6 0.9 broadcast_in_dim.16
  116.5 3.5 %all-to-all-start.6 = ((s16[4,16,8,640]{3,2,1,0:T(8,128)(2,1)}), s16[4,16,8,640]{3,2,1,0:T(8,128)(2,1)S(1)}, u32[]{:S(2)}, u32[]{:S(2)}) async-start(s16[4,16,8,640]{3,2,1,0:T(8,128)(2,1)} %broadcast_in_dim.16), calls=%async_computation.6 | async-start | bytes 1310720 | tf_op jit(solution)/shard_map/all_to_all | solution.py:115
  120.0 8.7 %all-to-all-done.6 = s16[4,16,8,640]{3,2,1,0:T(8,128)(2,1)S(1)} async-done(((s16[4,16,8,640]{3,2,1,0:T(8,128)(2,1)}), s16[4,16,8,640]{3,2,1,0:T(8,128)(2,1)S(1)}, u32[]{:S(2)}, u32[]{:S(2)}) %all-to-all-start.6) | async-done | bytes 655392 | tf_op jit(solution)/shard_map/all_to_all | solution.py:115
  128.7 0.2 convert_convert_fusion
  128.9 0.2 fusion.17
  129.1 0.2 fusion.3
  129.3 0.8 fusion
  130.1 0.3 fusion.6
  130.5 0.4 abs_reduce_fusion
  130.9 0.1 reshape.253
  131.0 0.2 fusion.14
  131.3 0.1 broadcast_in_dim.17
  131.4 20.7 %all_to_all.43 = s16[16,8,640]{2,1,0:T(8,128)(2,1)S(1)} all-to-all(s16[16,8,640]{2,1,0:T(8,128)(2,1)S(1)} %fusion.12), channel_id=1, replica_groups=mesh['z'=16,'y'=4,'fft'=8] {'z'}, dimensions={0} | all-to-all | bytes 327680 | tf_op jit(solution)/shard_map/all_to_all | solution.py:115
  152.1 0.2 copy.52
  152.3 0.1 fusion.15
  152.4 0.9 copy.61
  (24 shorter events, 0.4 us)
Async XLA Ops:
  33.5 13.5 %all-to-all-start.1 = ((bf16[4,16,8,640]{3,2,1,0:T(8,128)(2,1)}), bf16[4,16,8,640]{3,2,1,0:T(8,128)(2,1)S(1)}, u32[]{:S(2)}, u32[]{:S(2)}) async-start(bf16[4,16,8,640]{3,2,1,0:T(8,128)(2,1)} %broadcast_in_dim.13), calls=%async_computation.1 | async-start | bytes 1310720 | tf_op jit(solution)/shard_map/all_to_all | solution.py:115
  47.4 7.9 %copy-start = (f32[32,256]{1,0:T(8,128)S(1)}, f32[32,256]{1,0:T(8,128)}, u32[]{:S(2)}) copy-start(f32[32,256]{1,0:T(8,128)} %param.7) | copy-start | bytes 98308
  48.6 20.8 %all-to-all-start.2 = ((s16[16,8,640]{2,1,0:T(8,128)(2,1)}), s16[16,8,640]{2,1,0:T(8,128)(2,1)S(1)}, u32[]{:S(2)}, u32[]{:S(2)}) async-start(s16[16,8,640]{2,1,0:T(8,128)(2,1)} %fusion.11), calls=%async_computation.2 | async-start | bytes 327680 | tf_op jit(solution)/shard_map/all_to_all | solution.py:115
  95.9 19.7 %all-to-all-start.5 = ((s16[16,8,640]{2,1,0:T(8,128)(2,1)}), s16[16,8,640]{2,1,0:T(8,128)(2,1)S(1)}, u32[]{:S(2)}, u32[]{:S(2)}) async-start(s16[16,8,640]{2,1,0:T(8,128)(2,1)} %bitcast.18), calls=%async_computation.5 | async-start | bytes 327680 | tf_op jit(solution)/shard_map/all_to_all | solution.py:115
  116.5 12.2 %all-to-all-start.6 = ((s16[4,16,8,640]{3,2,1,0:T(8,128)(2,1)}), s16[4,16,8,640]{3,2,1,0:T(8,128)(2,1)S(1)}, u32[]{:S(2)}, u32[]{:S(2)}) async-start(s16[4,16,8,640]{3,2,1,0:T(8,128)(2,1)} %broadcast_in_dim.16), calls=%async_computation.6 | async-start | bytes 1310720 | tf_op jit(solution)/shard_map/all_to_all | solution.py:115

commit v3 on v2

--- a/solution.py
+++ b/solution.py
@@ -56,7 +56,7 @@
 
 def decoded_rows(codes, points):
     wide = from_16(codes)
-    return decoded(wide[..., :points], wide[..., points : points + 1])
+    return decoded(wide[..., :points], wide[..., points + 4 : points + 5])
 
 
 def halves(a):
@@ -116,7 +116,7 @@
 
 
 def to_all(x, axis):
-    return swap(jnp.broadcast_to(x[None], (lax.axis_size(axis), *x.shape)), axis)
+    return lax.all_gather(x, axis, axis=0, tiled=False)
 
 
 def pieces(slab):
@@ -141,11 +141,10 @@
     named = jnp.pad(named.astype(jnp.bfloat16), ((0, 0), (0, LANES - 4)))
     behind = jnp.broadcast_to(named[None], (Z, tasks, LANES))
     column = swap(jnp.concatenate([pieces(orbitals), behind], axis=2), "z")
-    every = to_all(column, "y").reshape(total, points + LANES)
-    table = every[:, :points]
+    table = to_all(column[:, :, :points], "y").reshape(total, points)
 
     def places(block):
-        names = block[:, points : points + 4].astype(jnp.int32)
+        names = block.reshape(-1, points + LANES)[:, points : points + 4].astype(jnp.int32)
         owner = names[:, :2].T.reshape(-1)
         return (owner % Y * Z + owner // Y) * orb_dev + names[:, 2:].T.reshape(-1)
 
@@ -153,17 +152,20 @@
         pick = place[:, None] == jnp.arange(total, dtype=jnp.int32)[None]
         return mul(pick.astype(jnp.bfloat16), table)
 
-    own = chosen(places(column.reshape(Z * tasks, points + LANES)))
+    own = chosen(places(column))
     density = coded_rows(own[: Z * tasks] * own[Z * tasks :])
     slab = whole(swap(density.reshape(Z, tasks, -1), "z"), width_y)
     weight = to_16(jnp.round((jnp.log(kernel) - KERNEL_MID) * (1.0 / KERNEL_STEP)))
     weight = jnp.broadcast_to(weight[None], (tasks, *weight.shape))
     full = swap(jnp.concatenate([slab, weight], axis=1), "fft")
     back = swap(potential_of(full), "fft")
-    spread = to_all(swap(pieces(back), "z"), "y").reshape(total, -1)
-    place = places(every)
+    spread = swap(pieces(back), "z")
+    lane = jnp.arange(points + LANES, dtype=jnp.int32)
+    beside = (lane >= points) & (lane < points + 4)
+    spread = to_all(jnp.where(beside, column.astype(jnp.int16), spread), "y")
+    place = places(spread)
     partner = chosen(jnp.concatenate([place[total:], place[:total]]))
-    potential = decoded_rows(spread, points)
+    potential = decoded_rows(spread.reshape(total, -1), points)
     contrib = (partner.reshape(2, total, points) * potential[None]).reshape(2 * total, points)
     mine = jnp.arange(Z * orb_dev, dtype=jnp.int32) + own_y * (Z * orb_dev)
     select = (mine[:, None] == place[None]).astype(jnp.bfloat16)

time: 154 us -> 150 us (0.974)
  blocking collectives: 72.6 us -> 97.5 us
  waiting for transfers between devices: 46.3 us -> 28.5 us
  starting transfers between devices: 19.3 us -> 9.14 us
    all_gather x0 -> x2, blocking collectives: none -> 27.9 us  [to_all(): return lax.all_gather(x, axis, axis=0, tiled=False)]
    all_to_all x4 -> x2, waiting for transfers between devices: 46.3 us -> 28.5 us  [swap(): return lax.all_to_all(x, axis, split_axis=0, concat_axis=0, tiled=True)]
    all_to_all x4 -> x2, starting transfers between devices: 19.3 us -> 9.14 us  [swap(): return lax.all_to_all(x, axis, split_axis=0, concat_axis=0, tiled=True)]
    all_to_all x4, blocking collectives: 72.6 us -> 69.7 us  [swap(): return lax.all_to_all(x, axis, split_axis=0, concat_axis=0, tiled=True)]
    broadcast_in_dim x2 -> x0, local copies, waits for them, and re-layouts: 1.78 us -> none  [to_all(): jnp.broadcast_to(x[None], (lax.axis_size(axis), *x.shape))]
  transfers between devices with their start and end apart: 4 -> 2, of which waited for: 4 -> 2; matrix products, arithmetic and copies ran while one was open for 0% -> 0% of each run, Pallas kernels for 0% -> 0%
where the time goes in v3:
time: 150 us; the launch traced here: 149 us
  blocking collectives  97.5 us (65%)
  waiting for transfers between devices  28.5 us (19%)
  starting transfers between devices  9.14 us (6%)
  local copies, waits for them, and re-layouts  4.2 us (3%)
  Pallas kernels  3.88 us (3%)
  other arithmetic  3.85 us (3%)
  matrix products  1.89 us (1%)
    all_to_all x4, blocking collectives, swap(): return lax.all_to_all(x, axis, split_axis=0, concat_axis=0, tiled=True)  69.7 us
    all_to_all x2, waiting for transfers between devices, swap(): return lax.all_to_all(x, axis, split_axis=0, concat_axis=0, tiled=True)  28.5 us
    all_gather x2, blocking collectives, to_all(): return lax.all_gather(x, axis, axis=0, tiled=False)  27.9 us
    all_to_all x2, starting transfers between devices, swap(): return lax.all_to_all(x, axis, split_axis=0, concat_axis=0, tiled=True)  9.14 us
    pallas_call x1, Pallas kernels, potential_of(): pl.pallas_call(transform_kernel, out_shape=jax.ShapeDtypeStruct((slabs, n...  3.88 us
  transfers between devices with their start and end apart: 2, of which 2 were waited for; matrix products, arithmetic and copies ran while one was open for 0% of the time, Pallas kernels for 0%

profile of v3, /device:TPU:32, one launch (start us, length us, event | category | flops | bytes accessed | tf_op | source)
XLA Modules:
  0.0 149.2 jit_solution(18085209566581766892)
XLA Ops:
  0.0 1.0 copy.46
  1.0 0.7 convert.7
  1.7 0.7 convert.8
  2.4 0.1 copy.60
  2.5 30.1 %all_to_all.30 = bf16[16,8,640]{2,1,0:T(8,128)(2,1)S(1)} all-to-all(bf16[16,8,640]{2,1,0:T(8,128)(2,1)S(1)} %pad_maximum_fusion), channel_id=1, replica_groups=mesh['z'=16,'y'=4,'fft'=8] {'z'}, dimensions={0} | all-to-all | bytes 327680 | tf_op jit(solution)/shard_map/all_to_all | solution.py:115
  32.6 0.0 copy-start
  32.7 14.0 %all-gather = bf16[64,8,512]{2,1,0:T(8,128)(2,1)S(1)} all-gather(bf16[16,8,512]{2,1,0:T(8,128)(2,1)S(1)} %slice.61), channel_id=2, replica_groups=mesh['z'=16,'y'=4,'fft'=8] {'y'}, dimensions={0}, use_global_device_ids=true | all-gather | bytes 655360 | tf_op jit(solution)/shard_map/all_gather | solution.py:119
  46.6 0.1 copy.59
  46.7 0.4 fusion.14
  47.1 0.1 abs_reduce_fusion.1
  47.2 0.2 fusion.18
  47.4 0.1 reshape.276
  47.5 0.1 broadcast_in_dim.13
  47.6 0.7 fusion.16
  48.3 4.8 %all-to-all-start.1 = ((s16[16,8,640]{2,1,0:T(8,128)(2,1)}), s16[16,8,640]{2,1,0:T(8,128)(2,1)S(1)}, u32[]{:S(2)}, u32[]{:S(2)}) async-start(s16[16,8,640]{2,1,0:T(8,128)(2,1)} %fusion.16), calls=%async_computation.1 | async-start | bytes 327680 | tf_op jit(solution)/shard_map/all_to_all | solution.py:115
  53.1 0.0 copy-done
  53.2 13.5 %all-to-all-done.1 = s16[16,8,640]{2,1,0:T(8,128)(2,1)S(1)} async-done(((s16[16,8,640]{2,1,0:T(8,128)(2,1)}), s16[16,8,640]{2,1,0:T(8,128)(2,1)S(1)}, u32[]{:S(2)}, u32[]{:S(2)}) %all-to-all-start.1) | async-done | bytes 163872 | tf_op jit(solution)/shard_map/all_to_all | solution.py:115
  66.8 12.1 %all_to_all.31.data_ref = s16[8,72,256]{2,1,0:T(8,128)(2,1)} all-to-all(s16[8,72,256]{2,1,0:T(8,128)(2,1)S(1)} %pad_add_fusion), channel_id=1, replica_groups=mesh['z'=16,'y'=4,'fft'=8] {'fft'}, dimensions={0} | all-to-all | bytes 589824 | tf_op jit(solution)/shard_map/all_to_all | solution.py:115
  78.8 3.9 %potential.1 = s16[8,40,256]{2,1,0:T(8,128)(2,1)} custom-call(s16[8,72,256]{2,1,0:T(8,128)(2,1)} %all_to_all.31.data_ref, bf16[256,512]{1,0:T(8,128)(2,1)} %constant.97.clone.cs_high, bf16[256,512]{1,0:T(8,128)(2,1)} %constant.98.clone.cs_low), custom_call_target="tpu_custom_call" | custom-call | tf_op jit(solution)/shard_map/potential/pallas_call | solution.py:107
  82.7 9.7 %all_to_all.32 = s16[8,40,256]{2,1,0:T(8,128)(2,1)S(1)} all-to-all(s16[8,40,256]{2,1,0:T(8,128)(2,1)} %potential.1), channel_id=1, replica_groups=mesh['z'=16,'y'=4,'fft'=8] {'fft'}, dimensions={0} | all-to-all | bytes 327680 | tf_op jit(solution)/shard_map/all_to_all | solution.py:115
  92.4 0.7 copy.50
  93.1 4.3 %all-to-all-start.4 = ((s16[16,8,640]{2,1,0:T(8,128)(2,1)}), s16[16,8,640]{2,1,0:T(8,128)(2,1)S(1)}, u32[]{:S(2)}, u32[]{:S(2)}) async-start(s16[16,8,640]{2,1,0:T(8,128)(2,1)} %bitcast.16), calls=%async_computation.4 | async-start | bytes 327680 | tf_op jit(solution)/shard_map/all_to_all | solution.py:115
  97.5 15.0 %all-to-all-done.4 = s16[16,8,640]{2,1,0:T(8,128)(2,1)S(1)} async-done(((s16[16,8,640]{2,1,0:T(8,128)(2,1)}), s16[16,8,640]{2,1,0:T(8,128)(2,1)S(1)}, u32[]{:S(2)}, u32[]{:S(2)}) %all-to-all-start.4) | async-done | bytes 163872 | tf_op jit(solution)/shard_map/all_to_all | solution.py:115
  112.5 0.1 convert_select_fusion
  112.6 13.9 %all-gather.1 = s16[64,8,640]{2,1,0:T(8,128)(2,1)S(1)} all-gather(s16[16,8,640]{2,1,0:T(8,128)(2,1)S(1)} %convert_select_fusion), channel_id=3, replica_groups=mesh['z'=16,'y'=4,'fft'=8] {'y'}, dimensions={0}, use_global_device_ids=true | all-gather | bytes 819200 | tf_op jit(solution)/shard_map/all_gather | solution.py:119
  126.5 0.5 copy.51
  127.1 0.2 convert_convert_fusion
  127.4 0.2 fusion.8
  127.6 0.3 copy.53
  127.9 0.8 fusion.4
  128.7 0.3 fusion
  129.0 0.3 fusion.11
  129.4 0.4 abs_reduce_fusion
  129.8 0.1 reshape.278
  129.9 0.2 fusion.19
  130.1 0.1 broadcast_in_dim.16
  130.2 17.8 %all_to_all.33 = s16[16,8,640]{2,1,0:T(8,128)(2,1)S(1)} all-to-all(s16[16,8,640]{2,1,0:T(8,128)(2,1)S(1)} %fusion.17), channel_id=1, replica_groups=mesh['z'=16,'y'=4,'fft'=8] {'z'}, dimensions={0} | all-to-all | bytes 327680 | tf_op jit(solution)/shard_map/all_to_all | solution.py:115
  148.0 0.1 fusion.26
  148.1 0.2 copy.57
  148.3 0.1 fusion.20
  148.4 0.9 copy.66
  (28 shorter events, 0.4 us)
Async XLA Ops:
  32.6 20.5 %copy-start = (f32[32,256]{1,0:T(8,128)S(1)}, f32[32,256]{1,0:T(8,128)}, u32[]{:S(2)}) copy-start(f32[32,256]{1,0:T(8,128)} %param.7) | copy-start | bytes 98308
  48.3 18.3 %all-to-all-start.1 = ((s16[16,8,640]{2,1,0:T(8,128)(2,1)}), s16[16,8,640]{2,1,0:T(8,128)(2,1)S(1)}, u32[]{:S(2)}, u32[]{:S(2)}) async-start(s16[16,8,640]{2,1,0:T(8,128)(2,1)} %fusion.16), calls=%async_computation.1 | async-start | bytes 327680 | tf_op jit(solution)/shard_map/all_to_all | solution.py:115
  93.1 19.4 %all-to-all-start.4 = ((s16[16,8,640]{2,1,0:T(8,128)(2,1)}), s16[16,8,640]{2,1,0:T(8,128)(2,1)S(1)}, u32[]{:S(2)}, u32[]{:S(2)}) async-start(s16[16,8,640]{2,1,0:T(8,128)(2,1)} %bitcast.16), calls=%async_computation.4 | async-start | bytes 327680 | tf_op jit(solution)/shard_map/all_to_all | solution.py:115

commit v4 on v2

v4 whole, which is shorter than its diff:
```python
import math

import jax
import jax.numpy as jnp
import numpy as np
from jax import lax
from jax.experimental import pallas as pl
from jax.experimental.pallas import tpu as pltpu
from jax.sharding import Mesh
from jax.sharding import PartitionSpec as P

Z, Y = 16, 4
LANES = 128
TOP = 32767.0
STEPS = 128.0
FLOOR = 1e-37
KERNEL_LOW, KERNEL_HIGH = 0.02, 2.0
KERNEL_MID = 0.5 * (math.log(KERNEL_HIGH) + math.log(KERNEL_LOW))
KERNEL_STEP = 0.5 * (math.log(KERNEL_HIGH) - math.log(KERNEL_LOW)) / TOP


def tables(length):
    series = np.arange(length, dtype=np.int64)
    angle = (series[:, None] * series[None, :] % length) * (2.0 * math.pi / length)
    return np.cos(angle).astype(np.float32), np.sin(angle).astype(np.float32)


def level_of(largest):
    return jnp.ceil(jnp.log(jnp.maximum(largest, FLOOR)) * (STEPS / math.log(2.0))) + 1.0


def coded(values, level):
    share = jnp.sqrt(jnp.abs(values) * jnp.exp(level * (-math.log(2.0) / STEPS)))
    share = jnp.round(jnp.minimum(share, 1.0) * TOP)
    return jnp.where(values < 0, -share, share)


def decoded(codes, level):
    share = codes * (1.0 / TOP)
    return share * jnp.abs(share) * jnp.exp(level * (math.log(2.0) / STEPS))


def to_16(codes):
    return codes.astype(jnp.int32).astype(jnp.int16)


def from_16(codes):
    return codes.astype(jnp.int32).astype(jnp.float32)


def halves(a):
    high = a.astype(jnp.bfloat16)
    low = (a - high.astype(jnp.float32)).astype(jnp.bfloat16)
    return high, low


def mul(a, b):
    return jnp.dot(a, b, preferred_element_type=jnp.float32)


def mul3(a, b):
    return mul(a[0], b[0]) + (mul(a[0], b[1]) + mul(a[1], b[0]))


def transform_kernel(data_ref, cs_high, cs_low, out_ref):
    n = cs_high.shape[0]
    count, _, lanes = data_ref.shape
    depth = n * n // (count * lanes)
    halved = n // lanes

    def assembled(blocks):
        blocks = blocks.reshape(Y // halved, halved, count // Y, depth, lanes)
        sides = [
            jnp.concatenate(
                [blocks[upper, side][:, None] for upper in range(Y // halved)], axis=1
            ).reshape(n, lanes)
            for side in range(halved)
        ]
        return jnp.concatenate(sides, axis=1)

    codes = from_16(data_ref[:, :depth])
    level = from_16(data_ref[:, depth : 2 * depth])
    grid = assembled(decoded(codes, level))
    log_weight = assembled(from_16(data_ref[:, 2 * depth :]))
    weight = jnp.exp(log_weight * KERNEL_STEP + KERNEL_MID).T * (1.0 / (n * n))
    row = (cs_high[:, :], cs_low[:, :])
    cos = (cs_high[:, :n], cs_low[:, :n])
    sin = (cs_high[:, n:], cs_low[:, n:])
    u = halves(mul3(halves(grid), row))
    p = mul3(cos, u)
    q = mul3(sin, u)
    h_real = halves((p[:, :n] - q[:, n:]) * weight)
    h_imag = halves((p[:, n:] + q[:, :n]) * weight)
    g_real = halves(mul3(cos, h_real) + mul3(sin, h_imag))
    g_imag = halves(mul3(sin, h_real) - mul3(cos, h_imag))
    spread = mul3(g_real, cos) - mul3(g_imag, sin)
    level = level_of(jnp.max(jnp.abs(spread), axis=(0, 1), keepdims=True))
    codes = coded(spread, level).reshape(count // Y, Y // halved, depth, n)
    out_ref[:, depth:] = to_16(jnp.broadcast_to(level[None], (count, 8, lanes)))
    for upper in range(Y // halved):
        for side in range(halved):
            part = codes[:, upper, :, side * lanes : (side + 1) * lanes]
            start = (upper * halved + side) * (count // Y)
            out_ref[start : start + count // Y, :depth] = to_16(part)


def potential_of(data, n):
    count, height, lanes = data.shape
    both = np.concatenate(tables(n), axis=1)
    high = both.astype(jnp.bfloat16)
    low = (both - high.astype(np.float32)).astype(jnp.bfloat16)
    return pl.pallas_call(
        transform_kernel,
        out_shape=jax.ShapeDtypeStruct((count, height // 3 + 8, lanes), jnp.int16),
        name="potential",
    )(data, jnp.asarray(high), jnp.asarray(low))


def swap(x, axis):
    return lax.all_to_all(x, axis, split_axis=0, concat_axis=0, tiled=True)


def paired(codes, tail):
    n, rows, lanes = codes.shape
    tail = jnp.pad(tail, ((0, 0), (0, 0), (0, lanes - tail.shape[2])))
    return jnp.concatenate([codes.reshape(n, rows // 2, 2, lanes), tail[:, None]], axis=1)


def row_level(values):
    return level_of(jnp.max(jnp.abs(values), axis=-1, keepdims=True))


def with_levels(codes, level):
    n, rows, _ = codes.shape
    tail = level.reshape(n, rows // 2, 2).transpose(0, 2, 1)
    return paired(to_16(codes), to_16(tail))


def levels_of(message):
    n, pairs = message.shape[0], message.shape[1] - 1
    tail = message[:, pairs, :, :pairs].transpose(0, 2, 1)
    return tail.reshape(n, pairs * 2)


def codes_of(message):
    n, pairs, _, lanes = message.shape
    return message[:, : pairs - 1].reshape(n, (pairs - 1) * 2, lanes)


def on_device(orbitals, kernel, partner_owner, partner_local):
    orb_dev, rows_x, width_y = orbitals.shape
    tasks = partner_local.shape[0]
    peers = Z * Y
    total = peers * orb_dev
    fft = lax.axis_size("fft")
    sides = width_y // LANES
    cut = orbitals.reshape(orb_dev, Y // sides, Z, sides, LANES).transpose(2, 1, 3, 0, 4)
    named = jnp.concatenate([partner_owner[:, :, 0].T, partner_local.T], axis=1)
    named = jnp.broadcast_to(named.astype(jnp.bfloat16)[None], (peers, 2, 2 * tasks))
    first = swap(paired(cut.reshape(peers, orb_dev, LANES), named), ("z", "y"))
    table = codes_of(first).reshape(total, LANES)
    names = first[:, orb_dev // 2, :, : 2 * tasks].astype(jnp.int32)
    place = names[:, :, :tasks] * orb_dev + names[:, :, tasks:]
    place = place.transpose(1, 0, 2).reshape(2 * total)
    orbs = jnp.arange(total, dtype=jnp.int32)
    pick = (place[:, None] == orbs[None]).astype(jnp.bfloat16)
    chosen = mul(pick, table)
    left, right = chosen[:total], chosen[total:]
    density = left * right
    level = row_level(density)
    block = Y * tasks
    there = with_levels(coded(density, level).reshape(Z, block, LANES), level)
    there = swap(there, "z")
    codes = codes_of(there).transpose(1, 0, 2)
    level = jnp.broadcast_to(levels_of(there).T[:, :, None], codes.shape)
    weight = to_16(jnp.round((jnp.log(kernel) - KERNEL_MID) * (1.0 / KERNEL_STEP)))
    weight = weight.reshape(Y // sides, Z, sides, LANES).transpose(0, 2, 1, 3)
    own_y = lax.axis_index("y")
    weight = lax.dynamic_index_in_dim(weight.reshape(Y, Z, LANES), own_y, 0)
    weight = jnp.broadcast_to(weight, codes.shape)
    data = swap(jnp.concatenate([codes, level, weight], axis=1), ("y", "fft"))
    back = swap(potential_of(data, width_y), ("y", "fft"))
    level = jnp.broadcast_to(back[None, :, Z, :1], (Z, block, 1))
    codes = back[:, :Z].transpose(1, 0, 2)
    tail = level.reshape(Z, block // 2, 2).transpose(0, 2, 1)
    spread = swap(paired(codes, tail), "z")
    level = from_16(levels_of(spread)).reshape(total, 1)
    potential = decoded(from_16(codes_of(spread)).reshape(total, LANES), level)
    contrib = jnp.concatenate([potential * right, potential * left], axis=0)
    select = (orbs[:, None] == place[None]).astype(jnp.bfloat16)
    high = lax.reduce_precision(contrib, 8, 7)
    low = (contrib - high).astype(jnp.bfloat16)
    summed = -(mul(select, high.astype(jnp.bfloat16)) + mul(select, low))
    level = row_level(summed)
    home = with_levels(coded(summed, level).reshape(peers, orb_dev, LANES), level)
    home = swap(home, ("z", "y"))
    level = from_16(levels_of(home))[:, :, None]
    result = decoded(from_16(codes_of(home)), level)
    result = result.reshape(Z, Y // sides, sides, orb_dev, LANES).transpose(3, 1, 0, 2, 4)
    return result.reshape(orb_dev, rows_x, width_y)


def solution(mesh):
    devices = mesh.devices.reshape(Z, Y, mesh.devices.shape[1])
    fine = Mesh(devices, ("z", "y", "fft"))
    orb = ("z", "y")
    in_specs = (P(orb, "fft", None), P("fft", None), P(orb, None, None), P(orb, None))
    out_specs = P(orb, "fft", None)
    return jax.shard_map(
        on_device, mesh=fine, in_specs=in_specs, out_specs=out_specs, check_vma=False
    )
```

time: 154 us -> 142 us (0.922)
  the two profiles are of different devices: /device:TPU:32 before, /device:TPU:2 now
where the time goes in v4:
time: 142 us
  blocking collectives  108 us (76%)
  waiting for transfers between devices  13.3 us (9%)
  local copies, waits for them, and re-layouts  7.28 us (5%)
  other arithmetic  4.16 us (3%)
  Pallas kernels  3.95 us (3%)
  starting transfers between devices  3.51 us (2%)
  matrix products  1.54 us (1%)
    all_to_all x5, blocking collectives, swap(): return lax.all_to_all(x, axis, split_axis=0, concat_axis=0, tiled=True)  108 us
    all_to_all x1, waiting for transfers between devices, swap(): return lax.all_to_all(x, axis, split_axis=0, concat_axis=0, tiled=True)  13.3 us
    pallas_call x1, Pallas kernels, potential_of(): pl.pallas_call(transform_kernel, out_shape=jax.ShapeDtypeStruct((count, h...  3.95 us
    all_to_all x1, starting transfers between devices, swap(): return lax.all_to_all(x, axis, split_axis=0, concat_axis=0, tiled=True)  3.51 us
  transfers between devices with their start and end apart: 1, of which 1 were waited for; matrix products, arithmetic and copies ran while one was open for 0% of the time, Pallas kernels for 0%

profile of v4, /device:TPU:2, one launch (start us, length us, event | category | flops | bytes accessed | tf_op | source)
XLA Modules:
  0.0 142.0 jit_solution(5003878417797067743)
XLA Ops:
  0.0 0.7 convert_bitcast_fusion
  0.7 0.7 convert.10
  1.5 0.9 reshape.162
  2.5 0.2 copy.72
  2.6 0.2 pad_maximum_fusion.1
  2.9 37.5 %all_to_all.30 = bf16[64,5,2,128]{3,2,1,0:T(2,128)(2,1)S(1)} all-to-all(bf16[64,5,2,128]{3,2,1,0:T(2,128)(2,1)S(1)} %pad_maximum_fusion.1), channel_id=1, replica_groups=mesh['z'=16,'y'=4,'fft'=8] {'z','y'}, dimensions={0} | all-to-all | bytes 327680 | tf_op jit(solution)/shard_map/all_to_all | solution.py:120
  40.4 0.1 fusion.17
  40.6 0.1 eq.29
  40.7 0.1 slice.59
  40.8 0.5 fusion.2
  41.3 0.1 abs_reduce_fusion.1
  41.4 0.2 reshape.182
  41.6 0.2 fusion.10
  41.9 0.1 pad_bitcast_fusion.1
  42.0 0.3 copy.74
  42.3 0.8 pad_add_fusion.2
  43.1 3.5 %all-to-all-start.1 = ((s16[16,17,2,128]{3,2,1,0:T(2,128)(2,1)}), s16[16,17,2,128]{3,2,1,0:T(2,128)(2,1)S(1)}, u32[]{:S(2)}, u32[]{:S(2)}) async-start(s16[16,17,2,128]{3,2,1,0:T(2,128)(2,1)} %pad_add_fusion.2), calls=%async_computation.1 | async-start | bytes 278528 | tf_op jit(solution)/shard_map/all_to_all | solution.py:120
  46.7 13.3 %all-to-all-done.1 = s16[16,17,2,128]{3,2,1,0:T(2,128)(2,1)S(1)} async-done(((s16[16,17,2,128]{3,2,1,0:T(2,128)(2,1)}), s16[16,17,2,128]{3,2,1,0:T(2,128)(2,1)S(1)}, u32[]{:S(2)}, u32[]{:S(2)}) %all-to-all-start.1) | async-done | bytes 139296 | tf_op jit(solution)/shard_map/all_to_all | solution.py:120
  60.0 0.1 slice.62
  60.2 0.1 copy.76
  60.3 0.1 broadcast_in_dim.46
  60.5 15.1 %all_to_all.31.data_ref = s16[32,48,128]{2,1,0:T(8,128)(2,1)} all-to-all(s16[32,48,128]{2,1,0:T(8,128)(2,1)S(1)} %pad_add_fusion), channel_id=1, replica_groups=mesh['z'=16,'y'=4,'fft'=8] {'y','fft'}, dimensions={0} | all-to-all | bytes 786432 | tf_op jit(solution)/shard_map/all_to_all | solution.py:120
  75.6 4.0 %potential.1 = s16[32,24,128]{2,1,0:T(8,128)(2,1)} custom-call(s16[32,48,128]{2,1,0:T(8,128)(2,1)} %all_to_all.31.data_ref, bf16[256,512]{1,0:T(8,128)(2,1)} %constant.48.clone.cs_high, bf16[256,512]{1,0:T(8,128)(2,1)} %constant.49.clone.cs_low), custom_call_target="tpu_custom_call" | custom-call | tf_op jit(solution)/shard_map/potential/pallas_call | solution.py:112
  79.6 12.1 %all_to_all.32 = s16[32,24,128]{2,1,0:T(8,128)(2,1)S(1)} all-to-all(s16[32,24,128]{2,1,0:T(8,128)(2,1)} %potential.1), channel_id=1, replica_groups=mesh['z'=16,'y'=4,'fft'=8] {'y','fft'}, dimensions={0} | all-to-all | bytes 393216 | tf_op jit(solution)/shard_map/all_to_all | solution.py:120
  91.7 0.7 slice_reduce_fusion
  92.3 0.1 broadcast_in_dim.49
  92.4 0.1 copy.78
  92.6 0.1 copy.79
  92.7 17.9 %all_to_all.33 = s16[16,17,2,128]{3,2,1,0:T(2,128)(2,1)S(1)} all-to-all(s16[16,17,2,128]{3,2,1,0:T(2,128)(2,1)S(1)} %copy.79), channel_id=1, replica_groups=mesh['z'=16,'y'=4,'fft'=8] {'z'}, dimensions={0} | all-to-all | bytes 278528 | tf_op jit(solution)/shard_map/all_to_all | solution.py:120
  110.6 0.2 copy.80
  110.8 0.1 exp.40
  110.9 0.2 convert_multiply_fusion.1
  111.1 0.1 slice_multiply_fusion
  111.3 0.5 fusion
  111.7 0.6 abs_reduce_fusion
  112.3 0.2 reshape.183
  112.5 0.5 pad_bitcast_fusion
  113.0 1.4 %copy.81 = s16[64,1,2,128]{3,2,1,0:T(2,128)(2,1)S(1)} copy(s16[64,1,2,128]{2,3,0,1:T(8,128)(2,1)S(1)} %pad_bitcast_fusion) | data formatting | bytes 65536 | tf_op jit(solution)/shard_map/broadcast_in_dim | solution.py:126
  114.5 0.2 fusion.13
  114.7 0.2 pad_add_fusion.1
  114.9 25.3 %all_to_all.34 = s16[64,5,2,128]{3,2,1,0:T(2,128)(2,1)S(1)} all-to-all(s16[64,5,2,128]{3,2,1,0:T(2,128)(2,1)S(1)} %pad_add_fusion.1), channel_id=1, replica_groups=mesh['z'=16,'y'=4,'fft'=8] {'z','y'}, dimensions={0} | all-to-all | bytes 327680 | tf_op jit(solution)/shard_map/all_to_all | solution.py:120
  140.2 0.1 copy.89
  140.3 0.1 copy.86
  140.5 0.1 reshape.184
  140.6 0.2 convert_multiply_fusion
  140.8 0.1 fusion.15
  141.0 0.1 copy.85
  141.1 0.9 reshape.168
  (25 shorter events, 0.5 us)
Async XLA Ops:
  40.7 6.0 %copy-start = (f32[32,256]{1,0:T(8,128)S(1)}, f32[32,256]{1,0:T(8,128)}, u32[]{:S(2)}) copy-start(f32[32,256]{1,0:T(8,128)} %param.7) | copy-start | bytes 98308
  43.1 16.9 %all-to-all-start.1 = ((s16[16,17,2,128]{3,2,1,0:T(2,128)(2,1)}), s16[16,17,2,128]{3,2,1,0:T(2,128)(2,1)S(1)}, u32[]{:S(2)}, u32[]{:S(2)}) async-start(s16[16,17,2,128]{3,2,1,0:T(2,128)(2,1)} %pad_add_fusion.2), calls=%async_computation.1 | async-start | bytes 278528 | tf_op jit(solution)/shard_map/all_to_all | solution.py:120

commit v5 on v4

v5 whole, which is shorter than its diff:
```python
import math

import jax
import jax.numpy as jnp
import numpy as np
from jax import lax
from jax.experimental import pallas as pl
from jax.experimental.pallas import tpu as pltpu
from jax.sharding import Mesh
from jax.sharding import PartitionSpec as P

Z, Y = 16, 4
LANES = 128
TOP = 32767.0
STEPS = 128.0
FLOOR = 1e-37
KERNEL_LOW, KERNEL_HIGH = 0.02, 2.0
KERNEL_MID = 0.5 * (math.log(KERNEL_HIGH) + math.log(KERNEL_LOW))
KERNEL_STEP = 0.5 * (math.log(KERNEL_HIGH) - math.log(KERNEL_LOW)) / TOP


def tables(length):
    series = np.arange(length, dtype=np.int64)
    angle = (series[:, None] * series[None, :] % length) * (2.0 * math.pi / length)
    return np.cos(angle).astype(np.float32), np.sin(angle).astype(np.float32)


def level_of(largest):
    return jnp.ceil(jnp.log(jnp.maximum(largest, FLOOR)) * (STEPS / math.log(2.0))) + 1.0


def coded(values, level):
    share = jnp.sqrt(jnp.abs(values) * jnp.exp(level * (-math.log(2.0) / STEPS)))
    share = jnp.round(jnp.minimum(share, 1.0) * TOP)
    return jnp.where(values < 0, -share, share)


def decoded(codes, level):
    share = codes * (1.0 / TOP)
    return share * jnp.abs(share) * jnp.exp(level * (math.log(2.0) / STEPS))


def to_16(codes):
    return codes.astype(jnp.int32).astype(jnp.int16)


def from_16(codes):
    return codes.astype(jnp.int32).astype(jnp.float32)


def halves(a):
    high = a.astype(jnp.bfloat16)
    low = (a - high.astype(jnp.float32)).astype(jnp.bfloat16)
    return high, low


def mul(a, b):
    return jnp.dot(a, b, preferred_element_type=jnp.float32)


def mul3(a, b):
    return mul(a[0], b[0]) + (mul(a[0], b[1]) + mul(a[1], b[0]))


def lane_of(shape):
    return lax.broadcasted_iota(jnp.int32, shape, len(shape) - 1)


def row_level(values):
    return level_of(jnp.max(jnp.abs(values), axis=-1, keepdims=True))


def to_lanes(level, n):
    rows, lanes = level.shape
    split = level.reshape(n, rows // n // 2, 2, lanes)
    pair = lax.broadcasted_iota(jnp.int32, split.shape, 1)
    return jnp.sum(jnp.where(lane_of(split.shape) == pair, split, 0.0), axis=1)


def to_rows(tail, pairs):
    n, _, lanes = tail.shape
    rows = 2 * pairs
    spread = jnp.broadcast_to(tail[:, None], (n, pairs, 2, lanes)).reshape(n, rows, lanes)
    row = lax.broadcasted_iota(jnp.int32, spread.shape, 1)
    kept = jnp.where(lane_of(spread.shape) == row // 2, spread, 0.0)
    return jnp.sum(kept.reshape(n * rows, lanes), axis=1, keepdims=True)


def write_rows(out_ref, values):
    n, pairs = out_ref.shape[0], out_ref.shape[1] - 1
    lanes = values.shape[1]
    level = row_level(values)
    codes = coded(values, level)
    out_ref[:, :pairs] = to_16(codes.reshape(n, pairs, 2, lanes))
    wide = jnp.broadcast_to(level, values.shape)
    out_ref[:, pairs:] = to_16(to_lanes(wide, n)[:, None])


def read_rows(ref):
    n, pairs, lanes = ref.shape[0], ref.shape[1] - 1, ref.shape[3]
    codes = from_16(ref[:, :pairs]).reshape(n * pairs * 2, lanes)
    return decoded(codes, to_rows(from_16(ref[:, pairs]), pairs))


def pack_kernel(orb_ref, owner_ref, local_ref, out_ref):
    count, rows, width = orb_ref.shape
    half = rows // Z
    orbs = orb_ref[...].astype(jnp.float32)
    for side in range(width // LANES):
        part = jnp.swapaxes(orbs[:, :, side * LANES : (side + 1) * LANES], 0, 1)
        for upper in range(half):
            piece = part[upper * Z : (upper + 1) * Z].reshape(Z, count // 2, 2, LANES)
            out_ref[:, upper, side, : count // 2] = piece.astype(jnp.bfloat16)
    lane = lane_of((local_ref.shape[0], LANES))
    task = lax.broadcasted_iota(jnp.int32, lane.shape, 0)
    rows_of = []
    for c in range(2):
        names = owner_ref[:, c] * count + local_ref[:, c : c + 1] - 256
        spread = jnp.where(lane == task, jnp.broadcast_to(names, lane.shape), 0)
        rows_of.append(jnp.sum(spread.astype(jnp.float32), axis=0, keepdims=True))
    tail = jnp.concatenate(rows_of, axis=0).astype(jnp.bfloat16)
    shape = (Z, half, width // LANES, 1, 2, LANES)
    out_ref[:, :, :, count // 2 :] = jnp.broadcast_to(tail[None, None, None, None], shape)


def density_kernel(first_ref, there_ref, chosen_ref, place_ref):
    peers, pairs, _, lanes = first_ref.shape
    pairs = pairs - 1
    total = peers * pairs * 2
    table = first_ref[:, :pairs].astype(jnp.float32).reshape(total, lanes)
    tasks = total // peers
    group = lanes // tasks
    tails = first_ref[:, pairs].astype(jnp.float32).reshape(peers // group, group, 2, lanes)
    place = tails[:, 0]
    for s in range(1, group):
        place = place + pltpu.roll(tails[:, s], s * tasks, 2)
    place = place.reshape(2 * (peers // group), lanes) + 256.0
    place_ref[...] = place
    column = place.T
    orbs = lane_of((lanes, total)).astype(jnp.float32)
    sides = []
    for c in range(2):
        pick = [
            (orbs == column[:, 2 * j + c : 2 * j + c + 1]).astype(jnp.bfloat16)
            for j in range(total // lanes)
        ]
        sides.append(mul(jnp.concatenate(pick, axis=0), table.astype(jnp.bfloat16)))
        chosen_ref[c] = sides[c].astype(jnp.bfloat16)
    write_rows(there_ref, sides[0] * sides[1])


def onward_kernel(place_ref, there_ref, weight_ref, out_ref):
    depth, pairs, _, lanes = there_ref.shape
    pairs = pairs - 1
    block = 2 * pairs
    half = depth // 2
    codes = from_16(there_ref[:, :pairs]).reshape(depth, block, lanes)
    codes = jnp.swapaxes(codes, 0, 1).reshape(block, half, 2, lanes)
    out_ref[:, :half] = to_16(codes)
    level = from_16(there_ref[:, pairs]).reshape(2 * depth, lanes).T[:pairs]
    level = jnp.concatenate([level, jnp.zeros((pairs, lanes - 2 * depth), jnp.float32)], axis=1)
    level = jnp.broadcast_to(level[:, None, None], (pairs, 2, 2, lanes)).reshape(block, 2, lanes)
    out_ref[:, 2 * half :] = to_16(level[:, None])
    own = jnp.zeros((depth, lanes), jnp.float32)
    for upper in range(weight_ref.shape[0] // depth):
        for side in range(weight_ref.shape[1] // lanes):
            part = weight_ref[upper * depth : (upper + 1) * depth, side * lanes : (side + 1) * lanes]
            here = place_ref[0] == upper * (weight_ref.shape[1] // lanes) + side
            own = jnp.where(here, part, own)
    own = jnp.round((jnp.log(own) - KERNEL_MID) * (1.0 / KERNEL_STEP)).reshape(half, 2, lanes)
    out_ref[:, half : 2 * half] = jnp.broadcast_to(to_16(own)[None], (block, half, 2, lanes))


def transform_kernel(place_ref, data_ref, cs_high, cs_low, out_ref):
    n = cs_high.shape[0]
    count, _, _, lanes = data_ref.shape
    depth = n * n // (count * lanes)
    half = depth // 2
    halved = n // lanes

    def assembled(blocks):
        blocks = blocks.reshape(Y // halved, halved, count // Y, depth, lanes)
        sides = [
            jnp.concatenate(
                [blocks[upper, side][:, None] for upper in range(Y // halved)], axis=1
            ).reshape(n, lanes)
            for side in range(halved)
        ]
        return jnp.concatenate(sides, axis=1)

    codes = from_16(data_ref[:, :half]).reshape(count, depth, lanes)
    tail = from_16(data_ref[:, 2 * half, :1])
    tail = jnp.broadcast_to(tail, (count, depth, lanes))
    row = lax.broadcasted_iota(jnp.int32, tail.shape, 1)
    tail = jnp.where(lane_of(tail.shape) == 2 * row + place_ref[1], tail, 0.0)
    grid = assembled(decoded(codes, jnp.sum(tail, axis=2, keepdims=True)))
    log_weight = assembled(from_16(data_ref[:, half : 2 * half]).reshape(count, depth, lanes))
    weight = jnp.exp(log_weight * KERNEL_STEP + KERNEL_MID).T * (1.0 / (n * n))
    row = (cs_high[:, :], cs_low[:, :])
    cos = (cs_high[:, :n], cs_low[:, :n])
    sin = (cs_high[:, n:], cs_low[:, n:])
    u = halves(mul3(halves(grid), row))
    p = mul3(cos, u)
    q = mul3(sin, u)
    h_real = halves((p[:, :n] - q[:, n:]) * weight)
    h_imag = halves((p[:, n:] + q[:, :n]) * weight)
    g_real = halves(mul3(cos, h_real) + mul3(sin, h_imag))
    g_imag = halves(mul3(sin, h_real) - mul3(cos, h_imag))
    spread = mul3(g_real, cos) - mul3(g_imag, sin)
    level = level_of(jnp.max(jnp.abs(spread), axis=(0, 1), keepdims=True))
    codes = coded(spread, level).reshape(count // Y, Y // halved, depth, n)
    out_ref[:, half:] = to_16(jnp.broadcast_to(level[None, None], (count, 1, 2, lanes)))
    for upper in range(Y // halved):
        for side in range(halved):
            part = codes[:, upper, :, side * lanes : (side + 1) * lanes]
            start = (upper * halved + side) * (count // Y)
            part = part.reshape(count // Y, half, 2, lanes)
            out_ref[start : start + count // Y, :half] = to_16(part)


def return_kernel(back_ref, out_ref):
    block, half, _, lanes = back_ref.shape
    half = half - 1
    depth = 2 * half
    codes = from_16(back_ref[:, :half]).reshape(block, depth, lanes)
    codes = jnp.swapaxes(codes, 0, 1).reshape(depth, block // 2, 2, lanes)
    out_ref[:, : block // 2] = to_16(codes)
    level = from_16(back_ref[:, half, :1]).reshape(block, lanes)
    tail = to_lanes(level, 1)[:, None]
    out_ref[:, block // 2 :] = to_16(jnp.broadcast_to(tail, (depth, 1, 2, lanes)))


def exchange_kernel(spread_ref, chosen_ref, place_ref, out_ref):
    total, lanes = chosen_ref.shape[1:]
    potential = read_rows(spread_ref)
    orbs = lax.broadcasted_iota(jnp.int32, (total, lanes), 0).astype(jnp.float32)
    summed = jnp.zeros((total, 2 * lanes), jnp.float32)
    for c in range(2):
        contrib = potential * chosen_ref[1 - c].astype(jnp.float32)
        high, low = halves(contrib)
        select = [
            (orbs == place_ref[2 * j + c : 2 * j + c + 1]).astype(jnp.bfloat16)
            for j in range(total // lanes)
        ]
        summed += mul(jnp.concatenate(select, axis=1), jnp.concatenate([high, low], axis=1))
    write_rows(out_ref, -(summed[:, :lanes] + summed[:, lanes:]))


def home_kernel(home_ref, out_ref):
    count, rows, width = out_ref.shape
    values = read_rows(home_ref).reshape(Z, rows // Z, width // LANES, count, LANES)
    for upper in range(rows // Z):
        for side in range(width // LANES):
            part = jnp.swapaxes(values[:, upper, side], 0, 1)
            lanes = slice(side * LANES, (side + 1) * LANES)
            out_ref[:, upper * Z : (upper + 1) * Z, lanes] = part


def local(kernel, out, name, scalars=0):
    def call(*operands):
        specs = [pl.BlockSpec(memory_space=pltpu.SMEM)] * scalars
        specs += [pl.BlockSpec(memory_space=pltpu.VMEM)] * (len(operands) - scalars)
        return pl.pallas_call(kernel, out_shape=out, in_specs=specs, name=name)(*operands)

    return call


def message(n, pairs, dtype=jnp.int16):
    return jax.ShapeDtypeStruct((n, pairs, 2, LANES), dtype)


def swap(x, axis):
    return lax.all_to_all(x, axis, split_axis=0, concat_axis=0, tiled=True)


def on_device(orbitals, kernel, partner_owner, partner_local):
    orb_dev, rows_x, width_y = orbitals.shape
    tasks = partner_local.shape[0]
    peers = Z * Y
    total = peers * orb_dev
    block = Y * tasks
    sides = width_y // LANES
    here = jnp.stack([lax.axis_index("y"), lax.axis_index("fft") % 2])
    both = np.concatenate(tables(width_y), axis=1)
    high = both.astype(jnp.bfloat16)
    low = (both - high.astype(np.float32)).astype(jnp.bfloat16)
    shape = (Z, Y // sides, sides, orb_dev // 2 + 1, 2, LANES)
    packed = local(pack_kernel, jax.ShapeDtypeStruct(shape, jnp.bfloat16), "pack")(
        orbitals, partner_owner, partner_local
    )
    first = swap(packed.reshape(peers, *shape[3:]), ("z", "y"))
    outs = (
        message(Z, block // 2 + 1),
        jax.ShapeDtypeStruct((2, total, LANES), jnp.bfloat16),
        jax.ShapeDtypeStruct((2 * total // LANES, LANES), jnp.float32),
    )
    there, chosen, place = local(density_kernel, outs, "density")(first)
    there = swap(there, "z")
    there = local(onward_kernel, message(block, Z + 1), "onward", 1)(here, there, kernel)
    there = swap(there, ("y", "fft"))
    back = local(transform_kernel, message(block, Z // 2 + 1), "potential", 1)(
        here, there, jnp.asarray(high), jnp.asarray(low)
    )
    back = swap(back, ("y", "fft"))
    back = swap(local(return_kernel, message(Z, block // 2 + 1), "return")(back), "z")
    home = local(exchange_kernel, message(peers, orb_dev // 2 + 1), "exchange")(
        back, chosen, place
    )
    home = swap(home, ("z", "y"))
    result = jax.ShapeDtypeStruct(orbitals.shape, jnp.float32)
    return local(home_kernel, result, "home")(home)


def solution(mesh):
    devices = mesh.devices.reshape(Z, Y, mesh.devices.shape[1])
    fine = Mesh(devices, ("z", "y", "fft"))
    orb = ("z", "y")
    in_specs = (P(orb, "fft", None), P("fft", None), P(orb, None, None), P(orb, None))
    out_specs = P(orb, "fft", None)
    return jax.shard_map(
        on_device, mesh=fine, in_specs=in_specs, out_specs=out_specs, check_vma=False
    )
```

time: 142 us -> 147 us (1.035)
  Pallas kernels: 3.95 us -> 18.2 us
  local copies, waits for them, and re-layouts: 7.28 us -> 2.7 us
  other arithmetic: 4.16 us -> 0.6 us
  matrix products: 1.54 us -> 0 us
    pallas_call x1 -> x7, Pallas kernels: 3.95 us -> 18.2 us  [call(): pl.pallas_call(kernel, out_shape=out, in_specs=specs, name=name)(*operands)]
    broadcast_in_dim x12 -> x0, local copies, waits for them, and re-layouts: 2.81 us -> none  [the longest x6 2.44 us: paired(): tail[:, None]]
    unnamed x4 -> x6, local copies, waits for them, and re-layouts: 0.11 us -> 2.7 us
    reshape x3 -> x0, local copies, waits for them, and re-layouts: 1.87 us -> none  [the longest x1 0.94 us: on_device(): orbitals.reshape(orb_dev, Y // sides, Z, sides, LANES)]
    dot_general x3 -> x0, matrix products: 1.54 us -> none  [mul(): return jnp.dot(a, b, preferred_element_type=jnp.float32)]
where the time goes in v5:
time: 147 us
  blocking collectives  109 us (74%)
  Pallas kernels  18.2 us (12%)
  waiting for transfers between devices  12.8 us (9%)
  starting transfers between devices  3.51 us (2%)
  local copies, waits for them, and re-layouts  2.7 us (2%)
    all_to_all x5, blocking collectives, swap(): return lax.all_to_all(x, axis, split_axis=0, concat_axis=0, tiled=True)  109 us
    pallas_call x7, Pallas kernels, call(): pl.pallas_call(kernel, out_shape=out, in_specs=specs, name=name)(*operands)  18.2 us
    all_to_all x1, waiting for transfers between devices, swap(): return lax.all_to_all(x, axis, split_axis=0, concat_axis=0, tiled=True)  12.8 us
    all_to_all x1, starting transfers between devices, swap(): return lax.all_to_all(x, axis, split_axis=0, concat_axis=0, tiled=True)  3.51 us
  transfers between devices with their start and end apart: 1, of which 1 were waited for; matrix products, arithmetic and copies ran while one was open for 0% of the time, Pallas kernels for 0%

profile of v5, /device:TPU:2, one launch (start us, length us, event | category | flops | bytes accessed | tf_op | source)
XLA Modules:
  0.0 146.6 jit_solution(262417271920038451)
XLA Ops:
  0.0 0.0 copy-start.1
  0.0 1.4 copy.8.local_ref
  1.4 0.0 copy-done.1
  1.4 0.7 copy.7.owner_ref
  2.0 1.8 %pack.1 = bf16[16,2,2,5,2,128]{5,4,3,2,1,0:T(2,128)(2,1)} custom-call(bf16[8,32,256]{2,1,0:T(8,128)(2,1)} %orb_ref.1, s32[8,2,1]{2,1,0:T(2,128)} %copy.7.owner_ref, s32[8,2]{1,0:T(8,128)} %copy.8.local_ref), custom_call_target="tpu_custom_call" | custom-call | tf_op jit(solution)/shard_map/pack/pallas_call | solution.py:263
  3.9 37.8 %all_to_all.30.first_ref = bf16[64,5,2,128]{3,2,1,0:T(2,128)(2,1)} all-to-all(bf16[64,5,2,128]{3,2,1,0:T(2,128)(2,1)} %bitcast.3), channel_id=1, replica_groups=mesh['z'=16,'y'=4,'fft'=8] {'z','y'}, dimensions={0} | all-to-all | bytes 327680 | tf_op jit(solution)/shard_map/all_to_all | solution.py:273
  41.7 2.8 %density.1 = (s16[16,17,2,128]{3,2,1,0:T(2,128)(2,1)}, bf16[2,512,128]{2,1,0:T(8,128)(2,1)}, f32[8,128]{1,0:T(8,128)}) custom-call(bf16[64,5,2,128]{3,2,1,0:T(2,128)(2,1)} %all_to_all.30.first_ref), custom_call_target="tpu_custom_call" | custom-call | tf_op jit(solution)/shard_map/density/pallas_call | solution.py:263
  44.5 3.5 %all-to-all-start.1 = ((s16[16,17,2,128]{3,2,1,0:T(2,128)(2,1)}), s16[16,17,2,128]{3,2,1,0:T(2,128)(2,1)S(1)}, u32[]{:S(2)}, u32[]{:S(2)}) async-start(s16[16,17,2,128]{3,2,1,0:T(2,128)(2,1)} %get-tuple-element.8), calls=%async_computation.1 | async-start | bytes 278528 | tf_op jit(solution)/shard_map/all_to_all | solution.py:273
  48.0 0.6 pad_add_fusion.place_ref
  48.6 12.8 %all-to-all-done.1.there_ref = s16[16,17,2,128]{3,2,1,0:T(2,128)(2,1)S(1)} async-done(((s16[16,17,2,128]{3,2,1,0:T(2,128)(2,1)}), s16[16,17,2,128]{3,2,1,0:T(2,128)(2,1)S(1)}, u32[]{:S(2)}, u32[]{:S(2)}) %all-to-all-start.1) | async-done | bytes 139296 | tf_op jit(solution)/shard_map/all_to_all | solution.py:273
  61.4 0.0 copy-start
  61.4 0.7 copy-done
  62.0 2.0 %onward.1 = s16[32,17,2,128]{3,2,1,0:T(2,128)(2,1)} custom-call(s32[2]{0:T(128)} %pad_add_fusion.place_ref, s16[16,17,2,128]{3,2,1,0:T(2,128)(2,1)} %copy-done, f32[32,256]{1,0:T(8,128)} %weight_ref.1), custom_call_target="tpu_custom_call" | custom-call | tf_op jit(solution)/shard_map/onward/pallas_call | solution.py:263
  64.1 14.1 %all_to_all.31.data_ref = s16[32,17,2,128]{3,2,1,0:T(2,128)(2,1)} all-to-all(s16[32,17,2,128]{3,2,1,0:T(2,128)(2,1)} %onward.1), channel_id=1, replica_groups=mesh['z'=16,'y'=4,'fft'=8] {'y','fft'}, dimensions={0} | all-to-all | bytes 557056 | tf_op jit(solution)/shard_map/all_to_all | solution.py:273
  78.2 4.3 %potential.1 = s16[32,9,2,128]{3,2,1,0:T(2,128)(2,1)} custom-call(s32[2]{0:T(128)} %pad_add_fusion.place_ref, s16[32,17,2,128]{3,2,1,0:T(2,128)(2,1)} %all_to_all.31.data_ref, bf16[256,512]{1,0:T(8,128)(2,1)} %constant.25.clone.cs_high, bf16[256,512]{1,0:T(8,128)(2,1)} %constant.26.clone.cs_low), custom_call_target="tpu_custom_call" | custom-call | tf_op jit(solution)/shard_map/potential/pallas_call | solution.py:263
  82.5 12.5 %all_to_all.32.back_ref = s16[32,9,2,128]{3,2,1,0:T(2,128)(2,1)} all-to-all(s16[32,9,2,128]{3,2,1,0:T(2,128)(2,1)} %potential.1), channel_id=1, replica_groups=mesh['z'=16,'y'=4,'fft'=8] {'y','fft'}, dimensions={0} | all-to-all | bytes 294912 | tf_op jit(solution)/shard_map/all_to_all | solution.py:273
  94.9 1.8 %return.1 = s16[16,17,2,128]{3,2,1,0:T(2,128)(2,1)} custom-call(s16[32,9,2,128]{3,2,1,0:T(2,128)(2,1)} %all_to_all.32.back_ref), custom_call_target="tpu_custom_call" | custom-call | tf_op jit(solution)/shard_map/return/pallas_call | solution.py:263
  96.7 18.1 %all_to_all.33.spread_ref = s16[16,17,2,128]{3,2,1,0:T(2,128)(2,1)} all-to-all(s16[16,17,2,128]{3,2,1,0:T(2,128)(2,1)} %return.1), channel_id=1, replica_groups=mesh['z'=16,'y'=4,'fft'=8] {'z'}, dimensions={0} | all-to-all | bytes 278528 | tf_op jit(solution)/shard_map/all_to_all | solution.py:273
  114.8 3.4 %exchange.1 = s16[64,5,2,128]{3,2,1,0:T(2,128)(2,1)} custom-call(s16[16,17,2,128]{3,2,1,0:T(2,128)(2,1)} %all_to_all.33.spread_ref, bf16[2,512,128]{2,1,0:T(8,128)(2,1)} %get-tuple-element.9.chosen_ref, f32[8,128]{1,0:T(8,128)} %get-tuple-element.10.place_ref), custom_call_target="tpu_custom_call" | custom-call | tf_op jit(solution)/shard_map/exchange/pallas_call | solution.py:263
  118.2 26.3 %all_to_all.34.home_ref = s16[64,5,2,128]{3,2,1,0:T(2,128)(2,1)} all-to-all(s16[64,5,2,128]{3,2,1,0:T(2,128)(2,1)} %exchange.1), channel_id=1, replica_groups=mesh['z'=16,'y'=4,'fft'=8] {'z','y'}, dimensions={0} | all-to-all | bytes 327680 | tf_op jit(solution)/shard_map/all_to_all | solution.py:273
  144.5 2.0 %home.1 = f32[8,32,256]{2,1,0:T(8,128)} custom-call(s16[64,5,2,128]{3,2,1,0:T(2,128)(2,1)} %all_to_all.34.home_ref), custom_call_target="tpu_custom_call" | custom-call | tf_op jit(solution)/shard_map/home/pallas_call | solution.py:263
Async XLA Ops:
  0.0 1.4 copy-start.1
  44.5 16.9 %all-to-all-start.1 = ((s16[16,17,2,128]{3,2,1,0:T(2,128)(2,1)}), s16[16,17,2,128]{3,2,1,0:T(2,128)(2,1)S(1)}, u32[]{:S(2)}, u32[]{:S(2)}) async-start(s16[16,17,2,128]{3,2,1,0:T(2,128)(2,1)} %get-tuple-element.8), calls=%async_computation.1 | async-start | bytes 278528 | tf_op jit(solution)/shard_map/all_to_all | solution.py:273
  61.4 0.7 copy-start

commit v6 on v4

v6 whole, which is shorter than its diff:
```python
import math

import jax
import jax.numpy as jnp
import numpy as np
from jax import lax
from jax.experimental import pallas as pl
from jax.experimental.pallas import tpu as pltpu
from jax.sharding import Mesh
from jax.sharding import PartitionSpec as P

Z, Y = 16, 4
LANES = 128
TOP = 32767.0
STEPS = 128.0
FLOOR = 1e-37
KERNEL_LOW, KERNEL_HIGH = 0.02, 2.0
KERNEL_MID = 0.5 * (math.log(KERNEL_HIGH) + math.log(KERNEL_LOW))
KERNEL_STEP = 0.5 * (math.log(KERNEL_HIGH) - math.log(KERNEL_LOW)) / TOP


def tables(length):
    series = np.arange(length, dtype=np.int64)
    angle = (series[:, None] * series[None, :] % length) * (2.0 * math.pi / length)
    return np.cos(angle).astype(np.float32), np.sin(angle).astype(np.float32)


def level_of(largest):
    return jnp.ceil(jnp.log(jnp.maximum(largest, FLOOR)) * (STEPS / math.log(2.0))) + 1.0


def coded(values, level):
    share = jnp.sqrt(jnp.abs(values) * jnp.exp(level * (-math.log(2.0) / STEPS)))
    share = jnp.round(jnp.minimum(share, 1.0) * TOP)
    return jnp.where(values < 0, -share, share)


def decoded(codes, level):
    share = codes * (1.0 / TOP)
    return share * jnp.abs(share) * jnp.exp(level * (math.log(2.0) / STEPS))


def to_16(codes):
    return codes.astype(jnp.int32).astype(jnp.int16)


def from_16(codes):
    return codes.astype(jnp.int32).astype(jnp.float32)


def halves(a):
    high = a.astype(jnp.bfloat16)
    low = (a - high.astype(jnp.float32)).astype(jnp.bfloat16)
    return high, low


def mul(a, b):
    return jnp.dot(a, b, preferred_element_type=jnp.float32)


def mul3(a, b):
    return mul(a[0], b[0]) + (mul(a[0], b[1]) + mul(a[1], b[0]))


def lane_of(shape):
    return lax.broadcasted_iota(jnp.int32, shape, len(shape) - 1)


def transform_kernel(here_ref, data_ref, cs_high, cs_low, out_ref):
    n = cs_high.shape[0]
    count, _, _, lanes = data_ref.shape
    depth = n * n // (count * lanes)
    half = depth // 2
    halved = n // lanes

    def assembled(blocks):
        blocks = blocks.reshape(Y // halved, halved, count // Y, depth, lanes)
        sides = [
            jnp.concatenate(
                [blocks[upper, side][:, None] for upper in range(Y // halved)], axis=1
            ).reshape(n, lanes)
            for side in range(halved)
        ]
        return jnp.concatenate(sides, axis=1)

    codes = from_16(data_ref[:, :half]).reshape(count, depth, lanes)
    tail = from_16(data_ref[:, 2 * half, :1])
    tail = jnp.broadcast_to(tail, (count, depth, lanes))
    row = lax.broadcasted_iota(jnp.int32, tail.shape, 1)
    tail = jnp.where(lane_of(tail.shape) == row, tail, 0.0)
    grid = assembled(decoded(codes, jnp.sum(tail, axis=2, keepdims=True)))
    log_weight = assembled(from_16(data_ref[:, half : 2 * half]).reshape(count, depth, lanes))
    weight = jnp.exp(log_weight * KERNEL_STEP + KERNEL_MID).T * (1.0 / (n * n))
    row = (cs_high[:, :], cs_low[:, :])
    cos = (cs_high[:, :n], cs_low[:, :n])
    sin = (cs_high[:, n:], cs_low[:, n:])
    u = halves(mul3(halves(grid), row))
    p = mul3(cos, u)
    q = mul3(sin, u)
    h_real = halves((p[:, :n] - q[:, n:]) * weight)
    h_imag = halves((p[:, n:] + q[:, :n]) * weight)
    g_real = halves(mul3(cos, h_real) + mul3(sin, h_imag))
    g_imag = halves(mul3(sin, h_real) - mul3(cos, h_imag))
    spread = mul3(g_real, cos) - mul3(g_imag, sin)
    level = level_of(jnp.max(jnp.abs(spread), axis=(0, 1), keepdims=True))
    codes = coded(spread, level).reshape(count // Y, Y // halved, depth, n)
    pair = jnp.full((2, lanes), here_ref[0] // 2, jnp.int32)
    side = lax.broadcasted_iota(jnp.int32, (2, lanes), 0)
    kept = (lane_of((2, lanes)) == pair) & (side == here_ref[0] % 2)
    tail = jnp.where(kept, level, 0.0)
    out_ref[:, half:] = to_16(jnp.broadcast_to(tail[None, None], (count, 1, 2, lanes)))
    for upper in range(Y // halved):
        for side in range(halved):
            part = codes[:, upper, :, side * lanes : (side + 1) * lanes]
            start = (upper * halved + side) * (count // Y)
            part = part.reshape(count // Y, half, 2, lanes)
            out_ref[start : start + count // Y, :half] = to_16(part)


def potential_of(data, here, n):
    count, pairs, _, lanes = data.shape
    both = np.concatenate(tables(n), axis=1)
    high = both.astype(jnp.bfloat16)
    low = (both - high.astype(np.float32)).astype(jnp.bfloat16)
    vmem = pl.BlockSpec(memory_space=pltpu.VMEM)
    return pl.pallas_call(
        transform_kernel,
        out_shape=jax.ShapeDtypeStruct((count, pairs // 2 + 1, 2, lanes), jnp.int16),
        in_specs=[pl.BlockSpec(memory_space=pltpu.SMEM), vmem, vmem, vmem],
        name="potential",
    )(here, data, jnp.asarray(high), jnp.asarray(low))


def swap(x, axis):
    return lax.all_to_all(x, axis, split_axis=0, concat_axis=0, tiled=True)


def message(codes, *tails):
    n, rows, lanes = codes.shape
    return jnp.concatenate([codes.reshape(n, rows // 2, 2, lanes), *tails], axis=1)


def codes_of(x):
    n, pairs, _, lanes = x.shape
    return x[:, : pairs - 1].reshape(n, (pairs - 1) * 2, lanes)


def tail_sum(x):
    return jnp.sum(x[:, -1].astype(jnp.int32), axis=0).astype(jnp.int16)


def block_level(values):
    return level_of(jnp.max(jnp.abs(values), axis=(1, 2), keepdims=True))


def on_device(orbitals, kernel, partner_owner, partner_local):
    orb_dev, rows_x, width_y = orbitals.shape
    tasks = partner_local.shape[0]
    peers = Z * Y
    total = peers * orb_dev
    block = Y * tasks
    sides = width_y // LANES
    own_z, own_y = lax.axis_index("z"), lax.axis_index("y")
    own_task = (own_y * tasks + lax.axis_index("fft")).reshape(1)
    cut = orbitals.reshape(orb_dev, Y // sides, Z, sides, LANES).transpose(2, 1, 3, 0, 4)
    names = (partner_owner[:, :, 0] * orb_dev + partner_local - 256).astype(jnp.bfloat16)
    names = jnp.pad(names.T, ((0, 0), (0, LANES - tasks)))
    names = jnp.broadcast_to(names[None, None], (peers, 1, 2, LANES))
    first = swap(message(cut.reshape(peers, orb_dev, LANES), names), ("z", "y"))
    table = codes_of(first).reshape(total, LANES)
    place = first[:, -1, :, :tasks].astype(jnp.int32).transpose(1, 0, 2).reshape(2 * total) + 256
    orbs = jnp.arange(total, dtype=jnp.int32)
    pick = (place[:, None] == orbs[None]).astype(jnp.bfloat16)
    chosen = mul(pick, table)
    left, right = chosen[:total], chosen[total:]
    density = (left * right).reshape(Z, block, LANES)
    level = block_level(density)
    tail = jnp.where(jnp.arange(LANES)[None, None, None] == own_z, level[:, None], 0.0)
    tail = jnp.broadcast_to(tail, (Z, 1, 2, LANES))
    there = message(to_16(coded(density, level)), to_16(tail))
    weight = to_16(jnp.round((jnp.log(kernel) - KERNEL_MID) * (1.0 / KERNEL_STEP)))
    weight = weight.reshape(Y // sides, Z, sides, LANES).transpose(0, 2, 1, 3)
    weight = lax.dynamic_index_in_dim(weight.reshape(Y, Z // 2, 2, LANES), own_y, 0)
    there, weight, own_task = lax.optimization_barrier((there, weight, own_task))
    there = swap(there, "z")
    tail = jnp.broadcast_to(tail_sum(there)[None, None], (block, 1, 2, LANES))
    weight = jnp.broadcast_to(weight, (block, Z // 2, 2, LANES))
    there = swap(message(codes_of(there).transpose(1, 0, 2), weight, tail), ("y", "fft"))
    back = swap(potential_of(there, own_task, width_y), ("y", "fft"))
    tail = jnp.broadcast_to(tail_sum(back)[None, None], (Z, 1, 2, LANES))
    spread = swap(message(codes_of(back).transpose(1, 0, 2), tail), "z")
    level = spread[:, -1, :, : block // 2].transpose(0, 2, 1).reshape(total, 1)
    potential = decoded(from_16(codes_of(spread)).reshape(total, LANES), from_16(level))
    contrib = jnp.concatenate([potential * right, potential * left], axis=0)
    select = (orbs[:, None] == place[None]).astype(jnp.bfloat16)
    high = lax.reduce_precision(contrib, 8, 7)
    low = (contrib - high).astype(jnp.bfloat16)
    summed = -(mul(select, high.astype(jnp.bfloat16)) + mul(select, low))
    summed = summed.reshape(peers, orb_dev, LANES)
    level = block_level(summed)
    tail = jnp.broadcast_to(to_16(level)[:, None], (peers, 1, 2, LANES))
    home = swap(message(to_16(coded(summed, level)), tail), ("z", "y"))
    result = decoded(from_16(codes_of(home)), from_16(home[:, -1, :1]))
    result = result.reshape(Z, Y // sides, sides, orb_dev, LANES).transpose(3, 1, 0, 2, 4)
    return result.reshape(orb_dev, rows_x, width_y)


def solution(mesh):
    devices = mesh.devices.reshape(Z, Y, mesh.devices.shape[1])
    fine = Mesh(devices, ("z", "y", "fft"))
    orb = ("z", "y")
    in_specs = (P(orb, "fft", None), P("fft", None), P(orb, None, None), P(orb, None))
    out_specs = P(orb, "fft", None)
    return jax.shard_map(
        on_device, mesh=fine, in_specs=in_specs, out_specs=out_specs, check_vma=False
    )
```

time: 142 us -> 138 us (0.972)
  blocking collectives: 108 us -> 85.4 us
  starting transfers between devices: 3.51 us -> 18.7 us
  waiting for transfers between devices: 13.3 us -> 18.9 us
  local copies, waits for them, and re-layouts: 7.28 us -> 3.64 us
    all_to_all x5, blocking collectives: 108 us -> 85.4 us  [swap(): return lax.all_to_all(x, axis, split_axis=0, concat_axis=0, tiled=True)]
    all_to_all x1, starting transfers between devices: 3.51 us -> 18.7 us  [swap(): return lax.all_to_all(x, axis, split_axis=0, concat_axis=0, tiled=True)]
    all_to_all x1, waiting for transfers between devices: 13.3 us -> 18.9 us  [swap(): return lax.all_to_all(x, axis, split_axis=0, concat_axis=0, tiled=True)]
    broadcast_in_dim x12 -> x6, local copies, waits for them, and re-layouts: 2.81 us -> 0.24 us  [the longest x1 0.13 us: on_device(): tail = jnp.broadcast_to(to_16(level)[:, None], (peers, 1, 2, LANES))]
where the time goes in v6:
time: 138 us
  blocking collectives  85.4 us (62%)
  waiting for transfers between devices  18.9 us (14%)
  starting transfers between devices  18.7 us (14%)
  other arithmetic  4.82 us (3%)
  Pallas kernels  4.26 us (3%)
  local copies, waits for them, and re-layouts  3.64 us (3%)
  matrix products  1.54 us (1%)
    all_to_all x5, blocking collectives, swap(): return lax.all_to_all(x, axis, split_axis=0, concat_axis=0, tiled=True)  85.4 us
    all_to_all x1, waiting for transfers between devices, swap(): return lax.all_to_all(x, axis, split_axis=0, concat_axis=0, tiled=True)  18.9 us
    all_to_all x1, starting transfers between devices, swap(): return lax.all_to_all(x, axis, split_axis=0, concat_axis=0, tiled=True)  18.7 us
    pallas_call x1, Pallas kernels, potential_of(): pl.pallas_call(transform_kernel, out_shape=jax.ShapeDtypeStruct((count, p...  4.26 us
  transfers between devices with their start and end apart: 1, of which 1 were waited for; matrix products, arithmetic and copies ran while one was open for 0% of the time, Pallas kernels for 0%

profile of v6, /device:TPU:2, one launch (start us, length us, event | category | flops | bytes accessed | tf_op | source)
XLA Modules:
  0.0 137.6 jit_solution(14939096727145915268)
XLA Ops:
  0.0 0.0 copy-start.1
  0.0 0.7 broadcast_multiply_fusion
  0.7 0.9 reshape.224
  1.6 0.0 copy-start
  1.7 0.2 copy.56
  1.8 0.0 copy-done.1
  1.9 0.9 pad_maximum_fusion.1
  2.8 18.7 %all-to-all-start = ((bf16[64,5,2,128]{3,2,1,0:T(2,128)(2,1)}), bf16[64,5,2,128]{3,2,1,0:T(2,128)(2,1)S(1)}, u32[]{:S(2)}, u32[]{:S(2)}) async-start(bf16[64,5,2,128]{3,2,1,0:T(2,128)(2,1)} %pad_maximum_fusion.1), calls=%async_computation | async-start | bytes 327680 | tf_op jit(solution)/shard_map/all_to_all | solution.py:135
  21.5 0.0 copy-done
  21.6 18.9 %all-to-all-done = bf16[64,5,2,128]{3,2,1,0:T(2,128)(2,1)S(1)} async-done(((bf16[64,5,2,128]{3,2,1,0:T(2,128)(2,1)}), bf16[64,5,2,128]{3,2,1,0:T(2,128)(2,1)S(1)}, u32[]{:S(2)}, u32[]{:S(2)}) %all-to-all-start) | async-done | bytes 163872 | tf_op jit(solution)/shard_map/all_to_all | solution.py:135
  40.5 0.1 add.74
  40.6 0.1 slice.49
  40.7 0.5 fusion.2
  41.3 0.1 fusion.21
  41.5 0.1 lt.24
  41.5 0.1 reduce_max.24
  41.6 0.1 reduce_max.25
  41.7 0.1 convert_convert_fusion.1
  41.8 0.7 fusion.10
  42.5 0.1 pad_add_fusion.2
  42.7 16.7 %all_to_all.30 = s16[16,17,2,128]{3,2,1,0:T(2,128)(2,1)S(1)} all-to-all(s16[16,17,2,128]{3,2,1,0:T(2,128)(2,1)S(1)} %pad_add_fusion.2), channel_id=1, replica_groups=mesh['z'=16,'y'=4,'fft'=8] {'z'}, dimensions={0} | all-to-all | bytes 278528 | tf_op jit(solution)/shard_map/all_to_all | solution.py:135
  59.4 0.1 slice.52
  59.5 0.1 copy.59
  59.6 0.1 broadcast_in_dim.40
  59.7 0.3 pad_add_fusion
  59.9 13.5 %all_to_all.31.data_ref = s16[32,17,2,128]{3,2,1,0:T(2,128)(2,1)} all-to-all(s16[32,17,2,128]{3,2,1,0:T(2,128)(2,1)S(1)} %pad_add_fusion), channel_id=1, replica_groups=mesh['z'=16,'y'=4,'fft'=8] {'y','fft'}, dimensions={0} | all-to-all | bytes 557056 | tf_op jit(solution)/shard_map/all_to_all | solution.py:135
  73.4 4.3 %potential.1 = s16[32,9,2,128]{3,2,1,0:T(2,128)(2,1)} custom-call(s32[1]{0:T(128)} %bitcast.10.here_ref, s16[32,17,2,128]{3,2,1,0:T(2,128)(2,1)} %all_to_all.31.data_ref, bf16[256,512]{1,0:T(8,128)(2,1)} %constant.20.clone.cs_high, bf16[256,512]{1,0:T(8,128)(2,1)} %constant.21.clone.cs_low), custom_call_target="tpu_custom_call" | custom-call | tf_op jit(solution)/shard_map/potential/pallas_call | solution.py:126
  77.7 11.8 %all_to_all.32 = s16[32,9,2,128]{3,2,1,0:T(2,128)(2,1)S(1)} all-to-all(s16[32,9,2,128]{3,2,1,0:T(2,128)(2,1)} %potential.1), channel_id=1, replica_groups=mesh['z'=16,'y'=4,'fft'=8] {'y','fft'}, dimensions={0} | all-to-all | bytes 294912 | tf_op jit(solution)/shard_map/all_to_all | solution.py:135
  89.5 0.1 slice.54
  89.6 0.1 copy.60
  89.7 18.4 %all_to_all.33 = s16[16,17,2,128]{3,2,1,0:T(2,128)(2,1)S(1)} all-to-all(s16[16,17,2,128]{3,2,1,0:T(2,128)(2,1)S(1)} %copy.60), channel_id=1, replica_groups=mesh['z'=16,'y'=4,'fft'=8] {'z'}, dimensions={0} | all-to-all | bytes 278528 | tf_op jit(solution)/shard_map/all_to_all | solution.py:135
  108.1 0.2 copy.61
  108.3 0.1 exp.40
  108.4 0.2 convert_multiply_fusion.1
  108.6 0.1 slice_multiply_fusion
  108.8 0.5 fusion
  109.3 0.6 fusion.23
  109.8 0.1 reduce_max.36
  109.9 0.1 reduce_max.37
  110.1 0.1 lt.27
  110.2 0.7 fusion.13
  110.9 0.1 broadcast_in_dim.43
  111.0 0.2 pad_add_fusion.1
  111.2 25.1 %all_to_all.34 = s16[64,5,2,128]{3,2,1,0:T(2,128)(2,1)S(1)} all-to-all(s16[64,5,2,128]{3,2,1,0:T(2,128)(2,1)S(1)} %pad_add_fusion.1), channel_id=1, replica_groups=mesh['z'=16,'y'=4,'fft'=8] {'z','y'}, dimensions={0} | all-to-all | bytes 327680 | tf_op jit(solution)/shard_map/all_to_all | solution.py:135
  136.3 0.2 convert_multiply_fusion
  136.5 0.1 copy.63
  136.7 0.9 reshape.232
  (26 shorter events, 0.5 us)
Async XLA Ops:
  0.0 1.8 %copy-start.1 = (s32[8,2]{0,1:T(2,128)S(1)}, s32[8,2]{0,1:T(2,128)}, u32[]{:S(2)}) copy-start(s32[8,2]{0,1:T(2,128)} %param.9) | copy-start | bytes 196
  1.6 19.9 %copy-start = (f32[32,256]{1,0:T(8,128)S(1)}, f32[32,256]{1,0:T(8,128)}, u32[]{:S(2)}) copy-start(f32[32,256]{1,0:T(8,128)} %param.7) | copy-start | bytes 98308
  2.8 37.7 %all-to-all-start = ((bf16[64,5,2,128]{3,2,1,0:T(2,128)(2,1)}), bf16[64,5,2,128]{3,2,1,0:T(2,128)(2,1)S(1)}, u32[]{:S(2)}, u32[]{:S(2)}) async-start(bf16[64,5,2,128]{3,2,1,0:T(2,128)(2,1)} %pad_maximum_fusion.1), calls=%async_computation | async-start | bytes 327680 | tf_op jit(solution)/shard_map/all_to_all | solution.py:135

commit v7 on v5

v7 whole, which is shorter than its diff:
```python
import math

import jax
import jax.numpy as jnp
import numpy as np
from jax import lax
from jax.experimental import pallas as pl
from jax.experimental.pallas import tpu as pltpu
from jax.sharding import Mesh
from jax.sharding import PartitionSpec as P

Z, Y = 16, 4
LANES = 128
TOP = 32767.0
STEPS = 128.0
FLOOR = 1e-37
KERNEL_LOW, KERNEL_HIGH = 0.02, 2.0
KERNEL_MID = 0.5 * (math.log(KERNEL_HIGH) + math.log(KERNEL_LOW))
KERNEL_STEP = 0.5 * (math.log(KERNEL_HIGH) - math.log(KERNEL_LOW)) / TOP


def tables(length):
    series = np.arange(length, dtype=np.int64)
    angle = (series[:, None] * series[None, :] % length) * (2.0 * math.pi / length)
    return np.cos(angle).astype(np.float32), np.sin(angle).astype(np.float32)


def level_of(largest):
    return jnp.ceil(jnp.log(jnp.maximum(largest, FLOOR)) * (STEPS / math.log(2.0))) + 1.0


def coded(values, level):
    share = jnp.sqrt(jnp.abs(values) * jnp.exp(level * (-math.log(2.0) / STEPS)))
    share = jnp.round(jnp.minimum(share, 1.0) * TOP)
    return jnp.where(values < 0, -share, share)


def decoded(codes, level):
    share = codes * (1.0 / TOP)
    return share * jnp.abs(share) * jnp.exp(level * (math.log(2.0) / STEPS))


def to_16(codes):
    return codes.astype(jnp.int32).astype(jnp.int16)


def from_16(codes):
    return codes.astype(jnp.int32).astype(jnp.float32)


def halves(a):
    high = a.astype(jnp.bfloat16)
    low = (a - high.astype(jnp.float32)).astype(jnp.bfloat16)
    return high, low


def mul(a, b):
    return jnp.dot(a, b, preferred_element_type=jnp.float32)


def mul3(a, b):
    return mul(a[0], b[0]) + (mul(a[0], b[1]) + mul(a[1], b[0]))


def lane_of(shape):
    return lax.broadcasted_iota(jnp.int32, shape, len(shape) - 1)


def tail_sum(ref):
    return jnp.sum(ref[:, ref.shape[1] - 1].astype(jnp.int32), axis=0)


def turned(ref):
    n, pairs, _, lanes = ref.shape
    codes = ref[:, : pairs - 1].astype(jnp.int32).reshape(n, (pairs - 1) * 2, lanes)
    codes = jnp.swapaxes(codes, 0, 1).reshape((pairs - 1) * 2, n // 2, 2, lanes)
    return codes.astype(jnp.int16)


def block_level(values):
    return level_of(jnp.max(jnp.max(jnp.abs(values), axis=1, keepdims=True), axis=2, keepdims=True))


def pack_kernel(z_ref, y_ref, task_ref, orb_ref, owner_ref, local_ref, out_ref):
    count, rows, width = orb_ref.shape
    half = rows // Z
    orbs = orb_ref[...].astype(jnp.float32)
    for side in range(width // LANES):
        part = jnp.swapaxes(orbs[:, :, side * LANES : (side + 1) * LANES], 0, 1)
        for upper in range(half):
            piece = part[upper * Z : (upper + 1) * Z].reshape(Z, count // 2, 2, LANES)
            out_ref[:, upper, side, : count // 2] = piece.astype(jnp.bfloat16)
    names = (owner_ref[...] * count + local_ref[...] - 256).astype(jnp.float32)
    rest = jnp.zeros((2, LANES - names.shape[1]), jnp.float32)
    tail = jnp.concatenate([names, rest], axis=1).astype(jnp.bfloat16)
    shape = (Z, half, width // LANES, 1, 2, LANES)
    out_ref[:, :, :, count // 2 :] = jnp.broadcast_to(tail[None, None, None, None], shape)


def density_kernel(z_ref, first_ref, there_ref, chosen_ref, place_ref):
    peers, pairs, _, lanes = first_ref.shape
    pairs = pairs - 1
    total = peers * pairs * 2
    table = first_ref[:, :pairs].astype(jnp.float32).reshape(total, lanes).astype(jnp.bfloat16)
    tasks = total // peers
    group = lanes // tasks
    tails = first_ref[:, pairs].astype(jnp.float32).reshape(peers // group, group, 2, lanes)
    place = tails[:, 0]
    for s in range(1, group):
        place = place + pltpu.roll(tails[:, s], s * tasks, 2)
    place = place.reshape(2 * (peers // group), lanes) + 256.0
    place_ref[...] = place
    column = place.T
    orbs = lane_of((lanes, total)).astype(jnp.float32)
    sides = []
    for c in range(2):
        pick = [
            (orbs == column[:, 2 * j + c : 2 * j + c + 1]).astype(jnp.bfloat16)
            for j in range(total // lanes)
        ]
        sides.append(mul(jnp.concatenate(pick, axis=0), table))
        chosen_ref[c] = sides[c].astype(jnp.bfloat16)
    n, block = there_ref.shape[0], there_ref.shape[1] - 1
    density = (sides[0] * sides[1]).reshape(n, 2 * block, lanes)
    level = block_level(density)
    there_ref[:, :block] = to_16(coded(density, level).reshape(n, block, 2, lanes))
    shape = (n, 1, 2, lanes)
    tail = jnp.where(lane_of(shape) == z_ref[0], jnp.broadcast_to(level[:, None], shape), 0.0)
    there_ref[:, block:] = to_16(tail)


def onward_kernel(y_ref, there_ref, weight_ref, out_ref):
    depth, _, _, lanes = there_ref.shape
    block, half = out_ref.shape[0], depth // 2
    out_ref[:, :half] = turned(there_ref)
    tail = tail_sum(there_ref).astype(jnp.int16)
    out_ref[:, 2 * half :] = jnp.broadcast_to(tail[None, None], (block, 1, 2, lanes))
    own = jnp.zeros((depth, lanes), jnp.float32)
    halved = weight_ref.shape[1] // lanes
    for upper in range(weight_ref.shape[0] // depth):
        for side in range(halved):
            part = weight_ref[upper * depth : (upper + 1) * depth, side * lanes : (side + 1) * lanes]
            own = jnp.where(y_ref[0] == upper * halved + side, part, own)
    own = jnp.round((jnp.log(own) - KERNEL_MID) * (1.0 / KERNEL_STEP)).reshape(half, 2, lanes)
    out_ref[:, half : 2 * half] = jnp.broadcast_to(to_16(own)[None], (block, half, 2, lanes))


def transform_kernel(task_ref, data_ref, cs_high, cs_low, out_ref):
    n = cs_high.shape[0]
    count, _, _, lanes = data_ref.shape
    depth = n * n // (count * lanes)
    half = depth // 2
    halved = n // lanes

    def assembled(blocks):
        blocks = blocks.reshape(Y // halved, halved, count // Y, depth, lanes)
        sides = [
            jnp.concatenate(
                [blocks[upper, side][:, None] for upper in range(Y // halved)], axis=1
            ).reshape(n, lanes)
            for side in range(halved)
        ]
        return jnp.concatenate(sides, axis=1)

    codes = from_16(data_ref[:, :half]).reshape(count, depth, lanes)
    tail = from_16(data_ref[:, 2 * half, :1])
    tail = jnp.broadcast_to(tail, (count, depth, lanes))
    row = lax.broadcasted_iota(jnp.int32, tail.shape, 1)
    tail = jnp.where(lane_of(tail.shape) == row, tail, 0.0)
    grid = assembled(decoded(codes, jnp.sum(tail, axis=2, keepdims=True)))
    log_weight = assembled(from_16(data_ref[:, half : 2 * half]).reshape(count, depth, lanes))
    weight = jnp.exp(log_weight * KERNEL_STEP + KERNEL_MID).T * (1.0 / (n * n))
    row = (cs_high[:, :], cs_low[:, :])
    cos = (cs_high[:, :n], cs_low[:, :n])
    sin = (cs_high[:, n:], cs_low[:, n:])
    u = halves(mul3(halves(grid), row))
    p = mul3(cos, u)
    q = mul3(sin, u)
    h_real = halves((p[:, :n] - q[:, n:]) * weight)
    h_imag = halves((p[:, n:] + q[:, :n]) * weight)
    g_real = halves(mul3(cos, h_real) + mul3(sin, h_imag))
    g_imag = halves(mul3(sin, h_real) - mul3(cos, h_imag))
    spread = mul3(g_real, cos) - mul3(g_imag, sin)
    level = level_of(jnp.max(jnp.abs(spread), axis=(0, 1), keepdims=True))
    codes = coded(spread, level).reshape(count // Y, Y // halved, depth, n)
    pair = jnp.full((2, lanes), task_ref[0] // 2, jnp.int32)
    side = lax.broadcasted_iota(jnp.int32, (2, lanes), 0)
    kept = (lane_of((2, lanes)) == pair) & (side == task_ref[0] % 2)
    tail = jnp.where(kept, level, 0.0)
    out_ref[:, half:] = to_16(jnp.broadcast_to(tail[None, None], (count, 1, 2, lanes)))
    for upper in range(Y // halved):
        for side in range(halved):
            part = codes[:, upper, :, side * lanes : (side + 1) * lanes]
            start = (upper * halved + side) * (count // Y)
            part = part.reshape(count // Y, half, 2, lanes)
            out_ref[start : start + count // Y, :half] = to_16(part)


def return_kernel(back_ref, out_ref):
    half = out_ref.shape[1] - 1
    out_ref[:, :half] = turned(back_ref)
    tail = tail_sum(back_ref).astype(jnp.int16)
    out_ref[:, half:] = jnp.broadcast_to(tail[None, None], (out_ref.shape[0], 1, 2, tail.shape[1]))


def exchange_kernel(spread_ref, chosen_ref, place_ref, out_ref):
    total, lanes = chosen_ref.shape[1:]
    n, pairs = spread_ref.shape[0], spread_ref.shape[1] - 1
    tail = from_16(spread_ref[:, pairs])
    tail = jnp.broadcast_to(tail[:, None], (n, pairs, 2, lanes)).reshape(n, 2 * pairs, lanes)
    row = lax.broadcasted_iota(jnp.int32, tail.shape, 1)
    tail = jnp.where(lane_of(tail.shape) == row // 2, tail, 0.0).reshape(total, lanes)
    level = jnp.sum(tail, axis=1, keepdims=True)
    codes = from_16(spread_ref[:, :pairs]).reshape(total, lanes)
    potential = decoded(codes, level)
    orbs = lax.broadcasted_iota(jnp.int32, (total, lanes), 0).astype(jnp.float32)
    summed = jnp.zeros((total, 2 * lanes), jnp.float32)
    for c in range(2):
        contrib = potential * chosen_ref[1 - c].astype(jnp.float32)
        high, low = halves(contrib)
        select = [
            (orbs == place_ref[2 * j + c : 2 * j + c + 1]).astype(jnp.bfloat16)
            for j in range(total // lanes)
        ]
        summed += mul(jnp.concatenate(select, axis=1), jnp.concatenate([high, low], axis=1))
    peers, half = out_ref.shape[0], out_ref.shape[1] - 1
    summed = -(summed[:, :lanes] + summed[:, lanes:]).reshape(peers, 2 * half, lanes)
    level = block_level(summed)
    out_ref[:, :half] = to_16(coded(summed, level).reshape(peers, half, 2, lanes))
    out_ref[:, half:] = to_16(jnp.broadcast_to(level[:, None], (peers, 1, 2, lanes)))


def home_kernel(home_ref, out_ref):
    count, rows, width = out_ref.shape
    peers, half = home_ref.shape[0], home_ref.shape[1] - 1
    codes = from_16(home_ref[:, :half]).reshape(peers, 2 * half, LANES)
    values = decoded(codes, from_16(home_ref[:, half])[:, :1])
    values = values.reshape(Z, rows // Z, width // LANES, count, LANES)
    for upper in range(rows // Z):
        for side in range(width // LANES):
            part = jnp.swapaxes(values[:, upper, side], 0, 1)
            lanes = slice(side * LANES, (side + 1) * LANES)
            out_ref[:, upper * Z : (upper + 1) * Z, lanes] = part


def local(kernel, out, name, scalars=0):
    def call(*operands):
        specs = [pl.BlockSpec(memory_space=pltpu.SMEM)] * scalars
        specs += [pl.BlockSpec(memory_space=pltpu.VMEM)] * (len(operands) - scalars)
        params = pltpu.CompilerParams(vmem_limit_bytes=16 * 2**20)
        return pl.pallas_call(
            kernel, out_shape=out, in_specs=specs, compiler_params=params, name=name
        )(*operands)

    return call


def message(n, pairs, dtype=jnp.int16):
    return jax.ShapeDtypeStruct((n, pairs, 2, LANES), dtype)


def swap(x, axis):
    return lax.all_to_all(x, axis, split_axis=0, concat_axis=0, tiled=True)


def on_device(orbitals, kernel, partner_owner, partner_local):
    orb_dev, rows_x, width_y = orbitals.shape
    tasks = partner_local.shape[0]
    peers = Z * Y
    total = peers * orb_dev
    block = Y * tasks
    sides = width_y // LANES
    own_z, own_y = lax.axis_index("z").reshape(1), lax.axis_index("y").reshape(1)
    own_task = own_y * tasks + lax.axis_index("fft")
    both = np.concatenate(tables(width_y), axis=1)
    high = both.astype(jnp.bfloat16)
    low = (both - high.astype(np.float32)).astype(jnp.bfloat16)
    shape = (Z, Y // sides, sides, orb_dev // 2 + 1, 2, LANES)
    packed = local(pack_kernel, jax.ShapeDtypeStruct(shape, jnp.bfloat16), "pack", 3)(
        own_z, own_y, own_task, orbitals, partner_owner[:, :, 0].T, partner_local.T
    )
    first = swap(packed.reshape(peers, *shape[3:]), ("z", "y"))
    outs = (
        message(Z, block // 2 + 1),
        jax.ShapeDtypeStruct((2, total, LANES), jnp.bfloat16),
        jax.ShapeDtypeStruct((2 * total // LANES, LANES), jnp.float32),
    )
    there, chosen, place = local(density_kernel, outs, "density", 1)(own_z, first)
    there = swap(there, "z")
    there = local(onward_kernel, message(block, Z + 1), "onward", 1)(own_y, there, kernel)
    there = swap(there, ("y", "fft"))
    back = local(transform_kernel, message(block, Z // 2 + 1), "potential", 1)(
        own_task, there, jnp.asarray(high), jnp.asarray(low)
    )
    back = swap(back, ("y", "fft"))
    back = swap(local(return_kernel, message(Z, block // 2 + 1), "return")(back), "z")
    home = local(exchange_kernel, message(peers, orb_dev // 2 + 1), "exchange")(
        back, chosen, place
    )
    home = swap(home, ("z", "y"))
    result = jax.ShapeDtypeStruct(orbitals.shape, jnp.float32)
    return local(home_kernel, result, "home")(home)


def solution(mesh):
    devices = mesh.devices.reshape(Z, Y, mesh.devices.shape[1])
    fine = Mesh(devices, ("z", "y", "fft"))
    orb = ("z", "y")
    in_specs = (P(orb, "fft", None), P("fft", None), P(orb, None, None), P(orb, None))
    out_specs = P(orb, "fft", None)
    return jax.shard_map(
        on_device, mesh=fine, in_specs=in_specs, out_specs=out_specs, check_vma=False
    )
```

time: 147 us -> 132 us (0.90)
  blocking collectives: 109 us -> 123 us
  waiting for transfers between devices: 12.8 us -> 0 us
  Pallas kernels: 18.2 us -> 6.77 us
  starting transfers between devices: 3.51 us -> 0 us
    all_to_all x5 -> x6, blocking collectives: 109 us -> 123 us  [swap(): return lax.all_to_all(x, axis, split_axis=0, concat_axis=0, tiled=True)]
    all_to_all x1 -> x0, waiting for transfers between devices: 12.8 us -> none  [swap(): return lax.all_to_all(x, axis, split_axis=0, concat_axis=0, tiled=True)]
    pallas_call x7, Pallas kernels: 18.2 us -> 6.77 us  [call(): pl.pallas_call(kernel, out_shape=out, in_specs=specs, compiler_params=par...]
    all_to_all x1 -> x0, starting transfers between devices: 3.51 us -> none  [swap(): return lax.all_to_all(x, axis, split_axis=0, concat_axis=0, tiled=True)]
  transfers between devices with their start and end apart: 1 -> 0, of which waited for: 1 -> 0; matrix products, arithmetic and copies ran while one was open for 0% -> 0% of each run, Pallas kernels for 0% -> 0%
where the time goes in v7:
time: 132 us; the launch traced here: 131 us
  blocking collectives  123 us (93%)
  Pallas kernels  6.77 us (5%)
  local copies, waits for them, and re-layouts  1.62 us (1%)
    all_to_all x6, blocking collectives, swap(): return lax.all_to_all(x, axis, split_axis=0, concat_axis=0, tiled=True)  123 us
    pallas_call x7, Pallas kernels, call(): pl.pallas_call(kernel, out_shape=out, in_specs=specs, compiler_params=par...  6.77 us

profile of v7, /device:TPU:2, one launch (start us, length us, event | category | flops | bytes accessed | tf_op | source)
XLA Modules:
  0.0 131.1 jit_solution(15449330439954595519)
XLA Ops:
  0.0 0.0 copy-start.5
  0.0 0.0 copy-start.4
  0.0 0.7 copy-done.5
  0.7 0.0 copy-done.4
  0.7 0.0 copy-start.2
  0.7 0.9 copy-done.2
  1.6 0.2 pack.1
  1.8 37.5 %all_to_all.30.first_ref = bf16[64,5,2,128]{3,2,1,0:T(2,128)(2,1)S(1)} all-to-all(bf16[64,5,2,128]{3,2,1,0:T(2,128)(2,1)S(1)} %bitcast.8), channel_id=1, replica_groups=mesh['z'=16,'y'=4,'fft'=8] {'z','y'}, dimensions={0} | all-to-all | bytes 327680 | tf_op jit(solution)/shard_map/all_to_all | solution.py:263
  39.3 1.0 density.1
  40.3 0.0 copy-start.3
  40.4 16.7 %all_to_all.31.there_ref = s16[16,17,2,128]{3,2,1,0:T(2,128)(2,1)S(1)} all-to-all(s16[16,17,2,128]{3,2,1,0:T(2,128)(2,1)S(1)} %get-tuple-element.8), channel_id=1, replica_groups=mesh['z'=16,'y'=4,'fft'=8] {'z'}, dimensions={0} | all-to-all | bytes 278528 | tf_op jit(solution)/shard_map/all_to_all | solution.py:263
  57.1 0.0 copy-done.3
  57.1 0.2 onward.1
  57.3 0.0 copy-start
  57.3 0.0 copy-start.1
  57.3 13.5 %all_to_all.32.data_ref = s16[32,17,2,128]{3,2,1,0:T(2,128)(2,1)S(1)} all-to-all(s16[32,17,2,128]{3,2,1,0:T(2,128)(2,1)S(1)} %onward.1), channel_id=1, replica_groups=mesh['z'=16,'y'=4,'fft'=8] {'y','fft'}, dimensions={0} | all-to-all | bytes 557056 | tf_op jit(solution)/shard_map/all_to_all | solution.py:263
  70.8 0.0 copy-done
  70.8 0.0 copy-done.1
  70.8 2.5 %potential.1 = s16[32,9,2,128]{3,2,1,0:T(2,128)(2,1)S(1)} custom-call(s32[1]{0:T(128)S(6)} %add.7.task_ref, s16[32,17,2,128]{3,2,1,0:T(2,128)(2,1)S(1)} %all_to_all.32.data_ref, bf16[256,512]{1,0:T(8,128)(2,1)S(1)} %copy-done.1, bf16[256,512]{1,0:T(8,128)(2,1)S(1)} %copy-done), custom_call_target="tpu_custom_call" | custom-call | tf_op jit(solution)/shard_map/potential/pallas_call | solution.py:251
  73.3 11.5 %all_to_all.33.back_ref = s16[32,9,2,128]{3,2,1,0:T(2,128)(2,1)S(1)} all-to-all(s16[32,9,2,128]{3,2,1,0:T(2,128)(2,1)S(1)} %potential.1), channel_id=1, replica_groups=mesh['z'=16,'y'=4,'fft'=8] {'y','fft'}, dimensions={0} | all-to-all | bytes 294912 | tf_op jit(solution)/shard_map/all_to_all | solution.py:263
  84.9 0.1 return.1
  85.0 18.4 %all_to_all.34.spread_ref = s16[16,17,2,128]{3,2,1,0:T(2,128)(2,1)S(1)} all-to-all(s16[16,17,2,128]{3,2,1,0:T(2,128)(2,1)S(1)} %return.1), channel_id=1, replica_groups=mesh['z'=16,'y'=4,'fft'=8] {'z'}, dimensions={0} | all-to-all | bytes 278528 | tf_op jit(solution)/shard_map/all_to_all | solution.py:263
  103.4 1.6 %exchange.1 = s16[64,5,2,128]{3,2,1,0:T(2,128)(2,1)S(1)} custom-call(s16[16,17,2,128]{3,2,1,0:T(2,128)(2,1)S(1)} %all_to_all.34.spread_ref, bf16[2,512,128]{2,1,0:T(8,128)(2,1)S(1)} %get-tuple-element.9.chosen_ref, f32[8,128]{1,0:T(8,128)S(1)} %get-tuple-element.10.place_ref), custom_call_target="tpu_custom_call" | custom-call | tf_op jit(solution)/shard_map/exchange/pallas_call | solution.py:251
  105.0 25.1 %all_to_all.35.home_ref = s16[64,5,2,128]{3,2,1,0:T(2,128)(2,1)S(1)} all-to-all(s16[64,5,2,128]{3,2,1,0:T(2,128)(2,1)S(1)} %exchange.1), channel_id=1, replica_groups=mesh['z'=16,'y'=4,'fft'=8] {'z','y'}, dimensions={0} | all-to-all | bytes 327680 | tf_op jit(solution)/shard_map/all_to_all | solution.py:263
  130.1 1.1 home.1
Async XLA Ops:
  0.0 0.7 copy-start.5
  0.0 0.7 copy-start.4
  0.7 0.9 copy-start.2
  40.3 16.7 %copy-start.3 = (f32[32,256]{1,0:T(8,128)S(1)}, f32[32,256]{1,0:T(8,128)}, u32[]{:S(2)}) copy-start(f32[32,256]{1,0:T(8,128)} %weight_ref.1) | copy-start | bytes 98308
  57.3 13.5 %copy-start = (bf16[256,512]{1,0:T(8,128)(2,1)S(1)}, bf16[256,512]{1,0:T(8,128)(2,1)}, u32[]{:S(2)}) copy-start(bf16[256,512]{1,0:T(8,128)(2,1)} %constant.21.clone.cs_low) | copy-start | bytes 786436
  57.3 13.5 %copy-start.1 = (bf16[256,512]{1,0:T(8,128)(2,1)S(1)}, bf16[256,512]{1,0:T(8,128)(2,1)}, u32[]{:S(2)}) copy-start(bf16[256,512]{1,0:T(8,128)(2,1)} %constant.20.clone.cs_high) | copy-start | bytes 786436

commit v8 on v7

--- a/solution.py
+++ b/solution.py
@@ -81,7 +81,18 @@
     return level_of(jnp.max(jnp.max(jnp.abs(values), axis=1, keepdims=True), axis=2, keepdims=True))
 
 
-def pack_kernel(z_ref, y_ref, task_ref, orb_ref, owner_ref, local_ref, out_ref):
+def pack_kernel(z_ref, y_ref, task_ref, orb_hbm, owner_hbm, local_hbm, out_ref, *scratch):
+    orb_ref, owner_ref, local_ref, sems = scratch
+    loads = [
+        pltpu.make_async_copy(source, here, sems.at[i])
+        for i, (source, here) in enumerate(
+            ((owner_hbm, owner_ref), (local_hbm, local_ref), (orb_hbm, orb_ref))
+        )
+    ]
+    for load in loads:
+        load.start()
+    for load in loads:
+        load.wait()
     count, rows, width = orb_ref.shape
     half = rows // Z
     orbs = orb_ref[...].astype(jnp.float32)
@@ -108,10 +119,10 @@
     place = tails[:, 0]
     for s in range(1, group):
         place = place + pltpu.roll(tails[:, s], s * tasks, 2)
-    place = place.reshape(2 * (peers // group), lanes) + 256.0
+    place = place.reshape(2 * (peers // group), lanes)
     place_ref[...] = place
     column = place.T
-    orbs = lane_of((lanes, total)).astype(jnp.float32)
+    orbs = lane_of((lanes, total)).astype(jnp.float32) - 256.0
     sides = []
     for c in range(2):
         pick = [
@@ -213,13 +224,16 @@
     level = jnp.sum(tail, axis=1, keepdims=True)
     codes = from_16(spread_ref[:, :pairs]).reshape(total, lanes)
     potential = decoded(codes, level)
-    orbs = lax.broadcasted_iota(jnp.int32, (total, lanes), 0).astype(jnp.float32)
+    orbs = lax.broadcasted_iota(jnp.int32, (total, lanes), 0).astype(jnp.float32) - 256.0
+    orbs = orbs.astype(jnp.bfloat16)
+    one, zero = jnp.ones((), jnp.bfloat16), jnp.zeros((), jnp.bfloat16)
+    place = place_ref[...].astype(jnp.bfloat16)
     summed = jnp.zeros((total, 2 * lanes), jnp.float32)
     for c in range(2):
         contrib = potential * chosen_ref[1 - c].astype(jnp.float32)
         high, low = halves(contrib)
         select = [
-            (orbs == place_ref[2 * j + c : 2 * j + c + 1]).astype(jnp.bfloat16)
+            jnp.where(orbs == place[2 * j + c : 2 * j + c + 1], one, zero)
             for j in range(total // lanes)
         ]
         summed += mul(jnp.concatenate(select, axis=1), jnp.concatenate([high, low], axis=1))
@@ -230,26 +244,33 @@
     out_ref[:, half:] = to_16(jnp.broadcast_to(level[:, None], (peers, 1, 2, lanes)))
 
 
-def home_kernel(home_ref, out_ref):
+def home_kernel(home_ref, out_hbm, out_ref, sems):
     count, rows, width = out_ref.shape
     peers, half = home_ref.shape[0], home_ref.shape[1] - 1
     codes = from_16(home_ref[:, :half]).reshape(peers, 2 * half, LANES)
     values = decoded(codes, from_16(home_ref[:, half])[:, :1])
     values = values.reshape(Z, rows // Z, width // LANES, count, LANES)
+    stores = []
     for upper in range(rows // Z):
+        half = pl.ds(upper * Z, Z)
         for side in range(width // LANES):
             part = jnp.swapaxes(values[:, upper, side], 0, 1)
-            lanes = slice(side * LANES, (side + 1) * LANES)
-            out_ref[:, upper * Z : (upper + 1) * Z, lanes] = part
-
-
-def local(kernel, out, name, scalars=0):
+            out_ref[:, half, side * LANES : (side + 1) * LANES] = part
+        stores.append(
+            pltpu.make_async_copy(out_ref.at[:, half], out_hbm.at[:, half], sems.at[upper])
+        )
+        stores[upper].start()
+    for store in stores:
+        store.wait()
+
+
+def local(kernel, out, name, scalars=0, arrays=pltpu.VMEM, **more):
     def call(*operands):
         specs = [pl.BlockSpec(memory_space=pltpu.SMEM)] * scalars
-        specs += [pl.BlockSpec(memory_space=pltpu.VMEM)] * (len(operands) - scalars)
+        specs += [pl.BlockSpec(memory_space=arrays)] * (len(operands) - scalars)
         params = pltpu.CompilerParams(vmem_limit_bytes=16 * 2**20)
         return pl.pallas_call(
-            kernel, out_shape=out, in_specs=specs, compiler_params=params, name=name
+            kernel, out_shape=out, in_specs=specs, compiler_params=params, name=name, **more
         )(*operands)
 
     return call
@@ -276,7 +297,11 @@
     high = both.astype(jnp.bfloat16)
     low = (both - high.astype(np.float32)).astype(jnp.bfloat16)
     shape = (Z, Y // sides, sides, orb_dev // 2 + 1, 2, LANES)
-    packed = local(pack_kernel, jax.ShapeDtypeStruct(shape, jnp.bfloat16), "pack", 3)(
+    names = pltpu.VMEM((2, tasks), jnp.int32)
+    scratch = [pltpu.VMEM(orbitals.shape, orbitals.dtype), names, names]
+    scratch.append(pltpu.SemaphoreType.DMA((3,)))
+    packed = jax.ShapeDtypeStruct(shape, jnp.bfloat16)
+    packed = local(pack_kernel, packed, "pack", 3, pltpu.HBM, scratch_shapes=scratch)(
         own_z, own_y, own_task, orbitals, partner_owner[:, :, 0].T, partner_local.T
     )
     first = swap(packed.reshape(peers, *shape[3:]), ("z", "y"))
@@ -299,7 +324,9 @@
     )
     home = swap(home, ("z", "y"))
     result = jax.ShapeDtypeStruct(orbitals.shape, jnp.float32)
-    return local(home_kernel, result, "home")(home)
+    scratch = [pltpu.VMEM(orbitals.shape, jnp.float32), pltpu.SemaphoreType.DMA((rows_x // Z,))]
+    spec = pl.BlockSpec(memory_space=pltpu.HBM)
+    return local(home_kernel, result, "home", out_specs=spec, scratch_shapes=scratch)(home)
 
 
 def solution(mesh):

time: 132 us -> 132 us (level)
  no operation moved by 1% of the time
where the time goes in v8:
time: 132 us; the launch traced here: 131 us
  blocking collectives  123 us (93%)
  Pallas kernels  7 us (5%)
  local copies, waits for them, and re-layouts  1.62 us (1%)
    all_to_all x6, blocking collectives, swap(): return lax.all_to_all(x, axis, split_axis=0, concat_axis=0, tiled=True)  123 us
    pallas_call x7, Pallas kernels, call(): pl.pallas_call(kernel, out_shape=out, in_specs=specs, compiler_params=par...  7 us

profile of v8, /device:TPU:2, one launch (start us, length us, event | category | flops | bytes accessed | tf_op | source)
XLA Modules:
  0.0 131.4 jit_solution(15530988117449417968)
XLA Ops:
  0.0 0.0 copy-start.5
  0.0 0.0 copy-start.4
  0.0 0.7 copy-done.5
  0.7 0.0 copy-done.4
  0.7 0.0 copy-start.2
  0.7 0.9 copy-done.2
  1.6 0.3 pack.1
  1.9 37.5 %all_to_all.30.first_ref = bf16[64,5,2,128]{3,2,1,0:T(2,128)(2,1)S(1)} all-to-all(bf16[64,5,2,128]{3,2,1,0:T(2,128)(2,1)S(1)} %bitcast.8), channel_id=1, replica_groups=mesh['z'=16,'y'=4,'fft'=8] {'z','y'}, dimensions={0} | all-to-all | bytes 327680 | tf_op jit(solution)/shard_map/all_to_all | solution.py:284
  39.5 1.0 density.1
  40.5 0.0 copy-start.3
  40.5 16.7 %all_to_all.31.there_ref = s16[16,17,2,128]{3,2,1,0:T(2,128)(2,1)S(1)} all-to-all(s16[16,17,2,128]{3,2,1,0:T(2,128)(2,1)S(1)} %get-tuple-element.8), channel_id=1, replica_groups=mesh['z'=16,'y'=4,'fft'=8] {'z'}, dimensions={0} | all-to-all | bytes 278528 | tf_op jit(solution)/shard_map/all_to_all | solution.py:284
  57.2 0.0 copy-done.3
  57.2 0.2 onward.1
  57.5 0.0 copy-start
  57.5 0.0 copy-start.1
  57.5 13.5 %all_to_all.32.data_ref = s16[32,17,2,128]{3,2,1,0:T(2,128)(2,1)S(1)} all-to-all(s16[32,17,2,128]{3,2,1,0:T(2,128)(2,1)S(1)} %onward.1), channel_id=1, replica_groups=mesh['z'=16,'y'=4,'fft'=8] {'y','fft'}, dimensions={0} | all-to-all | bytes 557056 | tf_op jit(solution)/shard_map/all_to_all | solution.py:284
  71.0 0.0 copy-done
  71.0 0.0 copy-done.1
  71.0 2.5 %potential.1 = s16[32,9,2,128]{3,2,1,0:T(2,128)(2,1)S(1)} custom-call(s32[1]{0:T(128)S(6)} %add.7.task_ref, s16[32,17,2,128]{3,2,1,0:T(2,128)(2,1)S(1)} %all_to_all.32.data_ref, bf16[256,512]{1,0:T(8,128)(2,1)S(1)} %copy-done.1, bf16[256,512]{1,0:T(8,128)(2,1)S(1)} %copy-done), custom_call_target="tpu_custom_call" | custom-call | tf_op jit(solution)/shard_map/potential/pallas_call | solution.py:272
  73.5 11.5 %all_to_all.33.back_ref = s16[32,9,2,128]{3,2,1,0:T(2,128)(2,1)S(1)} all-to-all(s16[32,9,2,128]{3,2,1,0:T(2,128)(2,1)S(1)} %potential.1), channel_id=1, replica_groups=mesh['z'=16,'y'=4,'fft'=8] {'y','fft'}, dimensions={0} | all-to-all | bytes 294912 | tf_op jit(solution)/shard_map/all_to_all | solution.py:284
  85.0 0.1 return.1
  85.2 18.4 %all_to_all.34.spread_ref = s16[16,17,2,128]{3,2,1,0:T(2,128)(2,1)S(1)} all-to-all(s16[16,17,2,128]{3,2,1,0:T(2,128)(2,1)S(1)} %return.1), channel_id=1, replica_groups=mesh['z'=16,'y'=4,'fft'=8] {'z'}, dimensions={0} | all-to-all | bytes 278528 | tf_op jit(solution)/shard_map/all_to_all | solution.py:284
  103.5 1.7 %exchange.1 = s16[64,5,2,128]{3,2,1,0:T(2,128)(2,1)S(1)} custom-call(s16[16,17,2,128]{3,2,1,0:T(2,128)(2,1)S(1)} %all_to_all.34.spread_ref, bf16[2,512,128]{2,1,0:T(8,128)(2,1)S(1)} %get-tuple-element.9.chosen_ref, f32[8,128]{1,0:T(8,128)S(1)} %get-tuple-element.10.place_ref), custom_call_target="tpu_custom_call" | custom-call | tf_op jit(solution)/shard_map/exchange/pallas_call | solution.py:272
  105.3 25.1 %all_to_all.35.home_ref = s16[64,5,2,128]{3,2,1,0:T(2,128)(2,1)S(1)} all-to-all(s16[64,5,2,128]{3,2,1,0:T(2,128)(2,1)S(1)} %exchange.1), channel_id=1, replica_groups=mesh['z'=16,'y'=4,'fft'=8] {'z','y'}, dimensions={0} | all-to-all | bytes 327680 | tf_op jit(solution)/shard_map/all_to_all | solution.py:284
  130.3 1.0 home.1
Async XLA Ops:
  0.0 0.7 copy-start.5
  0.0 0.7 copy-start.4
  0.7 0.9 copy-start.2
  40.5 16.7 %copy-start.3 = (f32[32,256]{1,0:T(8,128)S(1)}, f32[32,256]{1,0:T(8,128)}, u32[]{:S(2)}) copy-start(f32[32,256]{1,0:T(8,128)} %weight_ref.1) | copy-start | bytes 98308
  57.5 13.5 %copy-start = (bf16[256,512]{1,0:T(8,128)(2,1)S(1)}, bf16[256,512]{1,0:T(8,128)(2,1)}, u32[]{:S(2)}) copy-start(bf16[256,512]{1,0:T(8,128)(2,1)} %constant.21.clone.cs_low) | copy-start | bytes 786436
  57.5 13.5 %copy-start.1 = (bf16[256,512]{1,0:T(8,128)(2,1)S(1)}, bf16[256,512]{1,0:T(8,128)(2,1)}, u32[]{:S(2)}) copy-start(bf16[256,512]{1,0:T(8,128)(2,1)} %constant.20.clone.cs_high) | copy-start | bytes 786436

commit v9 on v8

--- a/solution.py
+++ b/solution.py
@@ -119,10 +119,10 @@
     place = tails[:, 0]
     for s in range(1, group):
         place = place + pltpu.roll(tails[:, s], s * tasks, 2)
-    place = place.reshape(2 * (peers // group), lanes)
+    place = place.reshape(2 * (peers // group), lanes) + 256.0
     place_ref[...] = place
     column = place.T
-    orbs = lane_of((lanes, total)).astype(jnp.float32) - 256.0
+    orbs = lane_of((lanes, total)).astype(jnp.float32)
     sides = []
     for c in range(2):
         pick = [
@@ -224,16 +224,13 @@
     level = jnp.sum(tail, axis=1, keepdims=True)
     codes = from_16(spread_ref[:, :pairs]).reshape(total, lanes)
     potential = decoded(codes, level)
-    orbs = lax.broadcasted_iota(jnp.int32, (total, lanes), 0).astype(jnp.float32) - 256.0
-    orbs = orbs.astype(jnp.bfloat16)
-    one, zero = jnp.ones((), jnp.bfloat16), jnp.zeros((), jnp.bfloat16)
-    place = place_ref[...].astype(jnp.bfloat16)
+    orbs = lax.broadcasted_iota(jnp.int32, (total, lanes), 0).astype(jnp.float32)
     summed = jnp.zeros((total, 2 * lanes), jnp.float32)
     for c in range(2):
         contrib = potential * chosen_ref[1 - c].astype(jnp.float32)
         high, low = halves(contrib)
         select = [
-            jnp.where(orbs == place[2 * j + c : 2 * j + c + 1], one, zero)
+            (orbs == place_ref[2 * j + c : 2 * j + c + 1]).astype(jnp.bfloat16)
             for j in range(total // lanes)
         ]
         summed += mul(jnp.concatenate(select, axis=1), jnp.concatenate([high, low], axis=1))
@@ -297,12 +294,14 @@
     high = both.astype(jnp.bfloat16)
     low = (both - high.astype(np.float32)).astype(jnp.bfloat16)
     shape = (Z, Y // sides, sides, orb_dev // 2 + 1, 2, LANES)
+    far = (orbitals, partner_owner[:, :, 0].T, partner_local.T)
+    far = [pltpu.with_memory_space_constraint(x, pltpu.HBM) for x in far]
     names = pltpu.VMEM((2, tasks), jnp.int32)
     scratch = [pltpu.VMEM(orbitals.shape, orbitals.dtype), names, names]
     scratch.append(pltpu.SemaphoreType.DMA((3,)))
     packed = jax.ShapeDtypeStruct(shape, jnp.bfloat16)
     packed = local(pack_kernel, packed, "pack", 3, pltpu.HBM, scratch_shapes=scratch)(
-        own_z, own_y, own_task, orbitals, partner_owner[:, :, 0].T, partner_local.T
+        own_z, own_y, own_task, *far
     )
     first = swap(packed.reshape(peers, *shape[3:]), ("z", "y"))
     outs = (

time: 132 us -> 131 us (level)
  local copies, waits for them, and re-layouts: 1.62 us -> 0.02 us
    unnamed x12 -> x6, local copies, waits for them, and re-layouts: 1.62 us -> 0.02 us
where the time goes in v9:
time: 131 us; the launch traced here: 130 us
  blocking collectives  123 us (94%)
  Pallas kernels  7.69 us (6%)
    all_to_all x6, blocking collectives, swap(): return lax.all_to_all(x, axis, split_axis=0, concat_axis=0, tiled=True)  123 us
    pallas_call x7, Pallas kernels, call(): pl.pallas_call(kernel, out_shape=out, in_specs=specs, compiler_params=par...  7.69 us

profile of v9, /device:TPU:2, one launch (start us, length us, event | category | flops | bytes accessed | tf_op | source)
XLA Modules:
  0.0 130.5 jit_solution(13260428383032570245)
XLA Ops:
  0.0 1.1 pack.1
  1.1 37.5 %all_to_all.30.first_ref = bf16[64,5,2,128]{3,2,1,0:T(2,128)(2,1)S(1)} all-to-all(bf16[64,5,2,128]{3,2,1,0:T(2,128)(2,1)S(1)} %bitcast.8), channel_id=1, replica_groups=mesh['z'=16,'y'=4,'fft'=8] {'z','y'}, dimensions={0} | all-to-all | bytes 327680 | tf_op jit(solution)/shard_map/all_to_all | solution.py:281
  38.6 1.1 density.1
  39.7 0.0 copy-start.2
  39.7 16.7 %all_to_all.31.there_ref = s16[16,17,2,128]{3,2,1,0:T(2,128)(2,1)S(1)} all-to-all(s16[16,17,2,128]{3,2,1,0:T(2,128)(2,1)S(1)} %get-tuple-element.8), channel_id=1, replica_groups=mesh['z'=16,'y'=4,'fft'=8] {'z'}, dimensions={0} | all-to-all | bytes 278528 | tf_op jit(solution)/shard_map/all_to_all | solution.py:281
  56.4 0.0 copy-done.2
  56.4 0.2 onward.1
  56.6 0.0 copy-start
  56.7 0.0 copy-start.1
  56.7 13.5 %all_to_all.32.data_ref = s16[32,17,2,128]{3,2,1,0:T(2,128)(2,1)S(1)} all-to-all(s16[32,17,2,128]{3,2,1,0:T(2,128)(2,1)S(1)} %onward.1), channel_id=1, replica_groups=mesh['z'=16,'y'=4,'fft'=8] {'y','fft'}, dimensions={0} | all-to-all | bytes 557056 | tf_op jit(solution)/shard_map/all_to_all | solution.py:281
  70.2 0.0 copy-done
  70.2 0.0 copy-done.1
  70.2 2.5 %potential.1 = s16[32,9,2,128]{3,2,1,0:T(2,128)(2,1)S(1)} custom-call(s32[1]{0:T(128)S(6)} %add.7.task_ref, s16[32,17,2,128]{3,2,1,0:T(2,128)(2,1)S(1)} %all_to_all.32.data_ref, bf16[256,512]{1,0:T(8,128)(2,1)S(1)} %copy-done.1, bf16[256,512]{1,0:T(8,128)(2,1)S(1)} %copy-done), custom_call_target="tpu_custom_call" | custom-call | tf_op jit(solution)/shard_map/potential/pallas_call | solution.py:269
  72.7 11.5 %all_to_all.33.back_ref = s16[32,9,2,128]{3,2,1,0:T(2,128)(2,1)S(1)} all-to-all(s16[32,9,2,128]{3,2,1,0:T(2,128)(2,1)S(1)} %potential.1), channel_id=1, replica_groups=mesh['z'=16,'y'=4,'fft'=8] {'y','fft'}, dimensions={0} | all-to-all | bytes 294912 | tf_op jit(solution)/shard_map/all_to_all | solution.py:281
  84.2 0.1 return.1
  84.4 18.4 %all_to_all.34.spread_ref = s16[16,17,2,128]{3,2,1,0:T(2,128)(2,1)S(1)} all-to-all(s16[16,17,2,128]{3,2,1,0:T(2,128)(2,1)S(1)} %return.1), channel_id=1, replica_groups=mesh['z'=16,'y'=4,'fft'=8] {'z'}, dimensions={0} | all-to-all | bytes 278528 | tf_op jit(solution)/shard_map/all_to_all | solution.py:281
  102.7 1.6 %exchange.1 = s16[64,5,2,128]{3,2,1,0:T(2,128)(2,1)S(1)} custom-call(s16[16,17,2,128]{3,2,1,0:T(2,128)(2,1)S(1)} %all_to_all.34.spread_ref, bf16[2,512,128]{2,1,0:T(8,128)(2,1)S(1)} %get-tuple-element.9.chosen_ref, f32[8,128]{1,0:T(8,128)S(1)} %get-tuple-element.10.place_ref), custom_call_target="tpu_custom_call" | custom-call | tf_op jit(solution)/shard_map/exchange/pallas_call | solution.py:269
  104.4 25.1 %all_to_all.35.home_ref = s16[64,5,2,128]{3,2,1,0:T(2,128)(2,1)S(1)} all-to-all(s16[64,5,2,128]{3,2,1,0:T(2,128)(2,1)S(1)} %exchange.1), channel_id=1, replica_groups=mesh['z'=16,'y'=4,'fft'=8] {'z','y'}, dimensions={0} | all-to-all | bytes 327680 | tf_op jit(solution)/shard_map/all_to_all | solution.py:281
  129.4 1.0 home.1
Async XLA Ops:
  39.7 16.7 %copy-start.2 = (f32[32,256]{1,0:T(8,128)S(1)}, f32[32,256]{1,0:T(8,128)}, u32[]{:S(2)}) copy-start(f32[32,256]{1,0:T(8,128)} %weight_ref.1) | copy-start | bytes 98308
  56.6 13.5 %copy-start = (bf16[256,512]{1,0:T(8,128)(2,1)S(1)}, bf16[256,512]{1,0:T(8,128)(2,1)}, u32[]{:S(2)}) copy-start(bf16[256,512]{1,0:T(8,128)(2,1)} %constant.21.clone.cs_low) | copy-start | bytes 786436
  56.7 13.5 %copy-start.1 = (bf16[256,512]{1,0:T(8,128)(2,1)S(1)}, bf16[256,512]{1,0:T(8,128)(2,1)}, u32[]{:S(2)}) copy-start(bf16[256,512]{1,0:T(8,128)(2,1)} %constant.20.clone.cs_high) | copy-start | bytes 786436

commit v10 on v9

--- a/solution.py
+++ b/solution.py
@@ -112,7 +112,7 @@
     peers, pairs, _, lanes = first_ref.shape
     pairs = pairs - 1
     total = peers * pairs * 2
-    table = first_ref[:, :pairs].astype(jnp.float32).reshape(total, lanes).astype(jnp.bfloat16)
+    table = first_ref[:, :pairs].reshape(total, lanes)
     tasks = total // peers
     group = lanes // tasks
     tails = first_ref[:, pairs].astype(jnp.float32).reshape(peers // group, group, 2, lanes)
@@ -134,7 +134,7 @@
     n, block = there_ref.shape[0], there_ref.shape[1] - 1
     density = (sides[0] * sides[1]).reshape(n, 2 * block, lanes)
     level = block_level(density)
-    there_ref[:, :block] = to_16(coded(density, level).reshape(n, block, 2, lanes))
+    there_ref[:, :block] = to_16(coded(density, level)).reshape(n, block, 2, lanes)
     shape = (n, 1, 2, lanes)
     tail = jnp.where(lane_of(shape) == z_ref[0], jnp.broadcast_to(level[:, None], shape), 0.0)
     there_ref[:, block:] = to_16(tail)
@@ -173,13 +173,13 @@
         ]
         return jnp.concatenate(sides, axis=1)
 
-    codes = from_16(data_ref[:, :half]).reshape(count, depth, lanes)
+    codes = from_16(data_ref[:, :half].reshape(count, depth, lanes))
     tail = from_16(data_ref[:, 2 * half, :1])
     tail = jnp.broadcast_to(tail, (count, depth, lanes))
     row = lax.broadcasted_iota(jnp.int32, tail.shape, 1)
     tail = jnp.where(lane_of(tail.shape) == row, tail, 0.0)
     grid = assembled(decoded(codes, jnp.sum(tail, axis=2, keepdims=True)))
-    log_weight = assembled(from_16(data_ref[:, half : 2 * half]).reshape(count, depth, lanes))
+    log_weight = assembled(from_16(data_ref[:, half : 2 * half].reshape(count, depth, lanes)))
     weight = jnp.exp(log_weight * KERNEL_STEP + KERNEL_MID).T * (1.0 / (n * n))
     row = (cs_high[:, :], cs_low[:, :])
     cos = (cs_high[:, :n], cs_low[:, :n])
@@ -203,8 +203,8 @@
         for side in range(halved):
             part = codes[:, upper, :, side * lanes : (side + 1) * lanes]
             start = (upper * halved + side) * (count // Y)
-            part = part.reshape(count // Y, half, 2, lanes)
-            out_ref[start : start + count // Y, :half] = to_16(part)
+            part = to_16(part).reshape(count // Y, half, 2, lanes)
+            out_ref[start : start + count // Y, :half] = part
 
 
 def return_kernel(back_ref, out_ref):
@@ -222,7 +222,7 @@
     row = lax.broadcasted_iota(jnp.int32, tail.shape, 1)
     tail = jnp.where(lane_of(tail.shape) == row // 2, tail, 0.0).reshape(total, lanes)
     level = jnp.sum(tail, axis=1, keepdims=True)
-    codes = from_16(spread_ref[:, :pairs]).reshape(total, lanes)
+    codes = from_16(spread_ref[:, :pairs].reshape(total, lanes))
     potential = decoded(codes, level)
     orbs = lax.broadcasted_iota(jnp.int32, (total, lanes), 0).astype(jnp.float32)
     summed = jnp.zeros((total, 2 * lanes), jnp.float32)
@@ -237,14 +237,14 @@
     peers, half = out_ref.shape[0], out_ref.shape[1] - 1
     summed = -(summed[:, :lanes] + summed[:, lanes:]).reshape(peers, 2 * half, lanes)
     level = block_level(summed)
-    out_ref[:, :half] = to_16(coded(summed, level).reshape(peers, half, 2, lanes))
+    out_ref[:, :half] = to_16(coded(summed, level)).reshape(peers, half, 2, lanes)
     out_ref[:, half:] = to_16(jnp.broadcast_to(level[:, None], (peers, 1, 2, lanes)))
 
 
 def home_kernel(home_ref, out_hbm, out_ref, sems):
     count, rows, width = out_ref.shape
     peers, half = home_ref.shape[0], home_ref.shape[1] - 1
-    codes = from_16(home_ref[:, :half]).reshape(peers, 2 * half, LANES)
+    codes = from_16(home_ref[:, :half].reshape(peers, 2 * half, LANES))
     values = decoded(codes, from_16(home_ref[:, half])[:, :1])
     values = values.reshape(Z, rows // Z, width // LANES, count, LANES)
     stores = []

time: 131 us -> 131 us (level)
  no operation moved by 1% of the time
where the time goes in v10:
time: 131 us; the launch traced here: 130 us
  blocking collectives  123 us (94%)
  Pallas kernels  7.49 us (6%)
    all_to_all x6, blocking collectives, swap(): return lax.all_to_all(x, axis, split_axis=0, concat_axis=0, tiled=True)  123 us
    pallas_call x7, Pallas kernels, call(): pl.pallas_call(kernel, out_shape=out, in_specs=specs, compiler_params=par...  7.49 us

profile of v10, /device:TPU:2, one launch (start us, length us, event | category | flops | bytes accessed | tf_op | source)
XLA Modules:
  0.0 130.3 jit_solution(11876184572644225295)
XLA Ops:
  0.0 1.1 pack.1
  1.1 37.5 %all_to_all.30.first_ref = bf16[64,5,2,128]{3,2,1,0:T(2,128)(2,1)S(1)} all-to-all(bf16[64,5,2,128]{3,2,1,0:T(2,128)(2,1)S(1)} %bitcast.8), channel_id=1, replica_groups=mesh['z'=16,'y'=4,'fft'=8] {'z','y'}, dimensions={0} | all-to-all | bytes 327680 | tf_op jit(solution)/shard_map/all_to_all | solution.py:281
  38.6 1.0 density.1
  39.6 0.0 copy-start.2
  39.6 16.7 %all_to_all.31.there_ref = s16[16,17,2,128]{3,2,1,0:T(2,128)(2,1)S(1)} all-to-all(s16[16,17,2,128]{3,2,1,0:T(2,128)(2,1)S(1)} %get-tuple-element.8), channel_id=1, replica_groups=mesh['z'=16,'y'=4,'fft'=8] {'z'}, dimensions={0} | all-to-all | bytes 278528 | tf_op jit(solution)/shard_map/all_to_all | solution.py:281
  56.3 0.0 copy-done.2
  56.3 0.2 onward.1
  56.6 0.0 copy-start
  56.6 0.0 copy-start.1
  56.6 13.5 %all_to_all.32.data_ref = s16[32,17,2,128]{3,2,1,0:T(2,128)(2,1)S(1)} all-to-all(s16[32,17,2,128]{3,2,1,0:T(2,128)(2,1)S(1)} %onward.1), channel_id=1, replica_groups=mesh['z'=16,'y'=4,'fft'=8] {'y','fft'}, dimensions={0} | all-to-all | bytes 557056 | tf_op jit(solution)/shard_map/all_to_all | solution.py:281
  70.1 0.0 copy-done
  70.1 0.0 copy-done.1
  70.1 2.5 %potential.1 = s16[32,9,2,128]{3,2,1,0:T(2,128)(2,1)S(1)} custom-call(s32[1]{0:T(128)S(6)} %add.7.task_ref, s16[32,17,2,128]{3,2,1,0:T(2,128)(2,1)S(1)} %all_to_all.32.data_ref, bf16[256,512]{1,0:T(8,128)(2,1)S(1)} %copy-done.1, bf16[256,512]{1,0:T(8,128)(2,1)S(1)} %copy-done), custom_call_target="tpu_custom_call" | custom-call | tf_op jit(solution)/shard_map/potential/pallas_call | solution.py:269
  72.5 11.5 %all_to_all.33.back_ref = s16[32,9,2,128]{3,2,1,0:T(2,128)(2,1)S(1)} all-to-all(s16[32,9,2,128]{3,2,1,0:T(2,128)(2,1)S(1)} %potential.1), channel_id=1, replica_groups=mesh['z'=16,'y'=4,'fft'=8] {'y','fft'}, dimensions={0} | all-to-all | bytes 294912 | tf_op jit(solution)/shard_map/all_to_all | solution.py:281
  84.1 0.1 return.1
  84.2 18.4 %all_to_all.34.spread_ref = s16[16,17,2,128]{3,2,1,0:T(2,128)(2,1)S(1)} all-to-all(s16[16,17,2,128]{3,2,1,0:T(2,128)(2,1)S(1)} %return.1), channel_id=1, replica_groups=mesh['z'=16,'y'=4,'fft'=8] {'z'}, dimensions={0} | all-to-all | bytes 278528 | tf_op jit(solution)/shard_map/all_to_all | solution.py:281
  102.6 1.6 %exchange.1 = s16[64,5,2,128]{3,2,1,0:T(2,128)(2,1)S(1)} custom-call(s16[16,17,2,128]{3,2,1,0:T(2,128)(2,1)S(1)} %all_to_all.34.spread_ref, bf16[2,512,128]{2,1,0:T(8,128)(2,1)S(1)} %get-tuple-element.9.chosen_ref, f32[8,128]{1,0:T(8,128)S(1)} %get-tuple-element.10.place_ref), custom_call_target="tpu_custom_call" | custom-call | tf_op jit(solution)/shard_map/exchange/pallas_call | solution.py:269
  104.1 25.1 %all_to_all.35.home_ref = s16[64,5,2,128]{3,2,1,0:T(2,128)(2,1)S(1)} all-to-all(s16[64,5,2,128]{3,2,1,0:T(2,128)(2,1)S(1)} %exchange.1), channel_id=1, replica_groups=mesh['z'=16,'y'=4,'fft'=8] {'z','y'}, dimensions={0} | all-to-all | bytes 327680 | tf_op jit(solution)/shard_map/all_to_all | solution.py:281
  129.2 1.0 home.1
Async XLA Ops:
  39.6 16.7 %copy-start.2 = (f32[32,256]{1,0:T(8,128)S(1)}, f32[32,256]{1,0:T(8,128)}, u32[]{:S(2)}) copy-start(f32[32,256]{1,0:T(8,128)} %weight_ref.1) | copy-start | bytes 98308
  56.6 13.5 %copy-start = (bf16[256,512]{1,0:T(8,128)(2,1)S(1)}, bf16[256,512]{1,0:T(8,128)(2,1)}, u32[]{:S(2)}) copy-start(bf16[256,512]{1,0:T(8,128)(2,1)} %constant.21.clone.cs_low) | copy-start | bytes 786436
  56.6 13.5 %copy-start.1 = (bf16[256,512]{1,0:T(8,128)(2,1)S(1)}, bf16[256,512]{1,0:T(8,128)(2,1)}, u32[]{:S(2)}) copy-start(bf16[256,512]{1,0:T(8,128)(2,1)} %constant.20.clone.cs_high) | copy-start | bytes 786436

commit v11 on v10

--- a/solution.py
+++ b/solution.py
@@ -83,24 +83,25 @@
 
 def pack_kernel(z_ref, y_ref, task_ref, orb_hbm, owner_hbm, local_hbm, out_ref, *scratch):
     orb_ref, owner_ref, local_ref, sems = scratch
+    count, rows, width = orb_ref.shape
+    half = rows // Z
     loads = [
-        pltpu.make_async_copy(source, here, sems.at[i])
-        for i, (source, here) in enumerate(
-            ((owner_hbm, owner_ref), (local_hbm, local_ref), (orb_hbm, orb_ref))
-        )
+        pltpu.make_async_copy(orb_hbm.at[:, pl.ds(i * Z, Z)], orb_ref.at[:, pl.ds(i * Z, Z)], sems.at[i])
+        for i in range(half)
     ]
+    loads.append(pltpu.make_async_copy(owner_hbm, owner_ref, sems.at[half]))
+    loads.append(pltpu.make_async_copy(local_hbm, local_ref, sems.at[half + 1]))
     for load in loads:
         load.start()
-    for load in loads:
-        load.wait()
-    count, rows, width = orb_ref.shape
-    half = rows // Z
-    orbs = orb_ref[...].astype(jnp.float32)
-    for side in range(width // LANES):
-        part = jnp.swapaxes(orbs[:, :, side * LANES : (side + 1) * LANES], 0, 1)
-        for upper in range(half):
-            piece = part[upper * Z : (upper + 1) * Z].reshape(Z, count // 2, 2, LANES)
+    for upper in range(half):
+        loads[upper].wait()
+        orbs = orb_ref[:, upper * Z : (upper + 1) * Z].astype(jnp.float32)
+        for side in range(width // LANES):
+            part = jnp.swapaxes(orbs[:, :, side * LANES : (side + 1) * LANES], 0, 1)
+            piece = part.reshape(Z, count // 2, 2, LANES)
             out_ref[:, upper, side, : count // 2] = piece.astype(jnp.bfloat16)
+    loads[half].wait()
+    loads[half + 1].wait()
     names = (owner_ref[...] * count + local_ref[...] - 256).astype(jnp.float32)
     rest = jnp.zeros((2, LANES - names.shape[1]), jnp.float32)
     tail = jnp.concatenate([names, rest], axis=1).astype(jnp.bfloat16)
@@ -298,7 +299,7 @@
     far = [pltpu.with_memory_space_constraint(x, pltpu.HBM) for x in far]
     names = pltpu.VMEM((2, tasks), jnp.int32)
     scratch = [pltpu.VMEM(orbitals.shape, orbitals.dtype), names, names]
-    scratch.append(pltpu.SemaphoreType.DMA((3,)))
+    scratch.append(pltpu.SemaphoreType.DMA((rows_x // Z + 2,)))
     packed = jax.ShapeDtypeStruct(shape, jnp.bfloat16)
     packed = local(pack_kernel, packed, "pack", 3, pltpu.HBM, scratch_shapes=scratch)(
         own_z, own_y, own_task, *far

time: 131 us -> 131 us (level)
  no operation moved by 1% of the time
where the time goes in v11:
time: 131 us; the launch traced here: 130 us
  blocking collectives  123 us (94%)
  Pallas kernels  7.42 us (6%)
    all_to_all x6, blocking collectives, swap(): return lax.all_to_all(x, axis, split_axis=0, concat_axis=0, tiled=True)  123 us
    pallas_call x7, Pallas kernels, call(): pl.pallas_call(kernel, out_shape=out, in_specs=specs, compiler_params=par...  7.42 us

profile of v11, /device:TPU:2, one launch (start us, length us, event | category | flops | bytes accessed | tf_op | source)
XLA Modules:
  0.0 130.2 jit_solution(14294498901269208173)
XLA Ops:
  0.0 1.1 pack.1
  1.1 37.5 %all_to_all.30.first_ref = bf16[64,5,2,128]{3,2,1,0:T(2,128)(2,1)S(1)} all-to-all(bf16[64,5,2,128]{3,2,1,0:T(2,128)(2,1)S(1)} %bitcast.8), channel_id=1, replica_groups=mesh['z'=16,'y'=4,'fft'=8] {'z','y'}, dimensions={0} | all-to-all | bytes 327680 | tf_op jit(solution)/shard_map/all_to_all | solution.py:282
  38.6 1.0 density.1
  39.5 0.0 copy-start.2
  39.6 16.7 %all_to_all.31.there_ref = s16[16,17,2,128]{3,2,1,0:T(2,128)(2,1)S(1)} all-to-all(s16[16,17,2,128]{3,2,1,0:T(2,128)(2,1)S(1)} %get-tuple-element.8), channel_id=1, replica_groups=mesh['z'=16,'y'=4,'fft'=8] {'z'}, dimensions={0} | all-to-all | bytes 278528 | tf_op jit(solution)/shard_map/all_to_all | solution.py:282
  56.3 0.0 copy-done.2
  56.3 0.2 onward.1
  56.5 0.0 copy-start
  56.5 0.0 copy-start.1
  56.5 13.5 %all_to_all.32.data_ref = s16[32,17,2,128]{3,2,1,0:T(2,128)(2,1)S(1)} all-to-all(s16[32,17,2,128]{3,2,1,0:T(2,128)(2,1)S(1)} %onward.1), channel_id=1, replica_groups=mesh['z'=16,'y'=4,'fft'=8] {'y','fft'}, dimensions={0} | all-to-all | bytes 557056 | tf_op jit(solution)/shard_map/all_to_all | solution.py:282
  70.0 0.0 copy-done
  70.0 0.0 copy-done.1
  70.0 2.5 %potential.1 = s16[32,9,2,128]{3,2,1,0:T(2,128)(2,1)S(1)} custom-call(s32[1]{0:T(128)S(6)} %add.7.task_ref, s16[32,17,2,128]{3,2,1,0:T(2,128)(2,1)S(1)} %all_to_all.32.data_ref, bf16[256,512]{1,0:T(8,128)(2,1)S(1)} %copy-done.1, bf16[256,512]{1,0:T(8,128)(2,1)S(1)} %copy-done), custom_call_target="tpu_custom_call" | custom-call | tf_op jit(solution)/shard_map/potential/pallas_call | solution.py:270
  72.5 11.5 %all_to_all.33.back_ref = s16[32,9,2,128]{3,2,1,0:T(2,128)(2,1)S(1)} all-to-all(s16[32,9,2,128]{3,2,1,0:T(2,128)(2,1)S(1)} %potential.1), channel_id=1, replica_groups=mesh['z'=16,'y'=4,'fft'=8] {'y','fft'}, dimensions={0} | all-to-all | bytes 294912 | tf_op jit(solution)/shard_map/all_to_all | solution.py:282
  84.0 0.1 return.1
  84.2 18.4 %all_to_all.34.spread_ref = s16[16,17,2,128]{3,2,1,0:T(2,128)(2,1)S(1)} all-to-all(s16[16,17,2,128]{3,2,1,0:T(2,128)(2,1)S(1)} %return.1), channel_id=1, replica_groups=mesh['z'=16,'y'=4,'fft'=8] {'z'}, dimensions={0} | all-to-all | bytes 278528 | tf_op jit(solution)/shard_map/all_to_all | solution.py:282
  102.5 1.6 %exchange.1 = s16[64,5,2,128]{3,2,1,0:T(2,128)(2,1)S(1)} custom-call(s16[16,17,2,128]{3,2,1,0:T(2,128)(2,1)S(1)} %all_to_all.34.spread_ref, bf16[2,512,128]{2,1,0:T(8,128)(2,1)S(1)} %get-tuple-element.9.chosen_ref, f32[8,128]{1,0:T(8,128)S(1)} %get-tuple-element.10.place_ref), custom_call_target="tpu_custom_call" | custom-call | tf_op jit(solution)/shard_map/exchange/pallas_call | solution.py:270
  104.1 25.1 %all_to_all.35.home_ref = s16[64,5,2,128]{3,2,1,0:T(2,128)(2,1)S(1)} all-to-all(s16[64,5,2,128]{3,2,1,0:T(2,128)(2,1)S(1)} %exchange.1), channel_id=1, replica_groups=mesh['z'=16,'y'=4,'fft'=8] {'z','y'}, dimensions={0} | all-to-all | bytes 327680 | tf_op jit(solution)/shard_map/all_to_all | solution.py:282
  129.1 1.0 home.1
Async XLA Ops:
  39.5 16.7 %copy-start.2 = (f32[32,256]{1,0:T(8,128)S(1)}, f32[32,256]{1,0:T(8,128)}, u32[]{:S(2)}) copy-start(f32[32,256]{1,0:T(8,128)} %weight_ref.1) | copy-start | bytes 98308
  56.5 13.5 %copy-start = (bf16[256,512]{1,0:T(8,128)(2,1)S(1)}, bf16[256,512]{1,0:T(8,128)(2,1)}, u32[]{:S(2)}) copy-start(bf16[256,512]{1,0:T(8,128)(2,1)} %constant.21.clone.cs_low) | copy-start | bytes 786436
  56.5 13.5 %copy-start.1 = (bf16[256,512]{1,0:T(8,128)(2,1)S(1)}, bf16[256,512]{1,0:T(8,128)(2,1)}, u32[]{:S(2)}) copy-start(bf16[256,512]{1,0:T(8,128)(2,1)} %constant.20.clone.cs_high) | copy-start | bytes 786436

commit v12 on v10

--- a/solution.py
+++ b/solution.py
@@ -252,11 +252,11 @@
         half = pl.ds(upper * Z, Z)
         for side in range(width // LANES):
             part = jnp.swapaxes(values[:, upper, side], 0, 1)
-            out_ref[:, half, side * LANES : (side + 1) * LANES] = part
-        stores.append(
-            pltpu.make_async_copy(out_ref.at[:, half], out_hbm.at[:, half], sems.at[upper])
-        )
-        stores[upper].start()
+            lanes = pl.ds(side * LANES, LANES)
+            out_ref[:, half, lanes] = part
+            here, there = out_ref.at[:, half, lanes], out_hbm.at[:, half, lanes]
+            stores.append(pltpu.make_async_copy(here, there, sems.at[len(stores)]))
+            stores[-1].start()
     for store in stores:
         store.wait()
 
@@ -323,7 +323,7 @@
     )
     home = swap(home, ("z", "y"))
     result = jax.ShapeDtypeStruct(orbitals.shape, jnp.float32)
-    scratch = [pltpu.VMEM(orbitals.shape, jnp.float32), pltpu.SemaphoreType.DMA((rows_x // Z,))]
+    scratch = [pltpu.VMEM(orbitals.shape, jnp.float32), pltpu.SemaphoreType.DMA((Y,))]
     spec = pl.BlockSpec(memory_space=pltpu.HBM)
     return local(home_kernel, result, "home", out_specs=spec, scratch_shapes=scratch)(home)
 

time: 131 us -> 131 us (level)
  no operation moved by 1% of the time
where the time goes in v12:
time: 131 us; the launch traced here: 130 us
  blocking collectives  123 us (94%)
  Pallas kernels  7.54 us (6%)
    all_to_all x6, blocking collectives, swap(): return lax.all_to_all(x, axis, split_axis=0, concat_axis=0, tiled=True)  123 us
    pallas_call x7, Pallas kernels, call(): pl.pallas_call(kernel, out_shape=out, in_specs=specs, compiler_params=par...  7.54 us

profile of v12, /device:TPU:2, one launch (start us, length us, event | category | flops | bytes accessed | tf_op | source)
XLA Modules:
  0.0 130.3 jit_solution(4944742344930595025)
XLA Ops:
  0.0 1.1 pack.1
  1.1 37.5 %all_to_all.30.first_ref = bf16[64,5,2,128]{3,2,1,0:T(2,128)(2,1)S(1)} all-to-all(bf16[64,5,2,128]{3,2,1,0:T(2,128)(2,1)S(1)} %bitcast.8), channel_id=1, replica_groups=mesh['z'=16,'y'=4,'fft'=8] {'z','y'}, dimensions={0} | all-to-all | bytes 327680 | tf_op jit(solution)/shard_map/all_to_all | solution.py:281
  38.6 1.0 density.1
  39.6 0.0 copy-start.2
  39.6 16.7 %all_to_all.31.there_ref = s16[16,17,2,128]{3,2,1,0:T(2,128)(2,1)S(1)} all-to-all(s16[16,17,2,128]{3,2,1,0:T(2,128)(2,1)S(1)} %get-tuple-element.8), channel_id=1, replica_groups=mesh['z'=16,'y'=4,'fft'=8] {'z'}, dimensions={0} | all-to-all | bytes 278528 | tf_op jit(solution)/shard_map/all_to_all | solution.py:281
  56.3 0.0 copy-done.2
  56.3 0.2 onward.1
  56.6 0.0 copy-start
  56.6 0.0 copy-start.1
  56.6 13.5 %all_to_all.32.data_ref = s16[32,17,2,128]{3,2,1,0:T(2,128)(2,1)S(1)} all-to-all(s16[32,17,2,128]{3,2,1,0:T(2,128)(2,1)S(1)} %onward.1), channel_id=1, replica_groups=mesh['z'=16,'y'=4,'fft'=8] {'y','fft'}, dimensions={0} | all-to-all | bytes 557056 | tf_op jit(solution)/shard_map/all_to_all | solution.py:281
  70.1 0.0 copy-done
  70.1 0.0 copy-done.1
  70.1 2.5 %potential.1 = s16[32,9,2,128]{3,2,1,0:T(2,128)(2,1)S(1)} custom-call(s32[1]{0:T(128)S(6)} %add.7.task_ref, s16[32,17,2,128]{3,2,1,0:T(2,128)(2,1)S(1)} %all_to_all.32.data_ref, bf16[256,512]{1,0:T(8,128)(2,1)S(1)} %copy-done.1, bf16[256,512]{1,0:T(8,128)(2,1)S(1)} %copy-done), custom_call_target="tpu_custom_call" | custom-call | tf_op jit(solution)/shard_map/potential/pallas_call | solution.py:269
  72.5 11.5 %all_to_all.33.back_ref = s16[32,9,2,128]{3,2,1,0:T(2,128)(2,1)S(1)} all-to-all(s16[32,9,2,128]{3,2,1,0:T(2,128)(2,1)S(1)} %potential.1), channel_id=1, replica_groups=mesh['z'=16,'y'=4,'fft'=8] {'y','fft'}, dimensions={0} | all-to-all | bytes 294912 | tf_op jit(solution)/shard_map/all_to_all | solution.py:281
  84.1 0.1 return.1
  84.2 18.4 %all_to_all.34.spread_ref = s16[16,17,2,128]{3,2,1,0:T(2,128)(2,1)S(1)} all-to-all(s16[16,17,2,128]{3,2,1,0:T(2,128)(2,1)S(1)} %return.1), channel_id=1, replica_groups=mesh['z'=16,'y'=4,'fft'=8] {'z'}, dimensions={0} | all-to-all | bytes 278528 | tf_op jit(solution)/shard_map/all_to_all | solution.py:281
  102.6 1.6 %exchange.1 = s16[64,5,2,128]{3,2,1,0:T(2,128)(2,1)S(1)} custom-call(s16[16,17,2,128]{3,2,1,0:T(2,128)(2,1)S(1)} %all_to_all.34.spread_ref, bf16[2,512,128]{2,1,0:T(8,128)(2,1)S(1)} %get-tuple-element.9.chosen_ref, f32[8,128]{1,0:T(8,128)S(1)} %get-tuple-element.10.place_ref), custom_call_target="tpu_custom_call" | custom-call | tf_op jit(solution)/shard_map/exchange/pallas_call | solution.py:269
  104.1 25.1 %all_to_all.35.home_ref = s16[64,5,2,128]{3,2,1,0:T(2,128)(2,1)S(1)} all-to-all(s16[64,5,2,128]{3,2,1,0:T(2,128)(2,1)S(1)} %exchange.1), channel_id=1, replica_groups=mesh['z'=16,'y'=4,'fft'=8] {'z','y'}, dimensions={0} | all-to-all | bytes 327680 | tf_op jit(solution)/shard_map/all_to_all | solution.py:281
  129.2 1.1 home.1
Async XLA Ops:
  39.6 16.7 %copy-start.2 = (f32[32,256]{1,0:T(8,128)S(1)}, f32[32,256]{1,0:T(8,128)}, u32[]{:S(2)}) copy-start(f32[32,256]{1,0:T(8,128)} %weight_ref.1) | copy-start | bytes 98308
  56.6 13.5 %copy-start = (bf16[256,512]{1,0:T(8,128)(2,1)S(1)}, bf16[256,512]{1,0:T(8,128)(2,1)}, u32[]{:S(2)}) copy-start(bf16[256,512]{1,0:T(8,128)(2,1)} %constant.21.clone.cs_low) | copy-start | bytes 786436
  56.6 13.5 %copy-start.1 = (bf16[256,512]{1,0:T(8,128)(2,1)S(1)}, bf16[256,512]{1,0:T(8,128)(2,1)}, u32[]{:S(2)}) copy-start(bf16[256,512]{1,0:T(8,128)(2,1)} %constant.20.clone.cs_high) | copy-start | bytes 786436
